TPU v7x, 128 devices: a whole 4x4x4 slice. The times are simulated.
128 devices in a mesh: leaf: 16 (over y, z), front: 8 (over x, core).
Axes of the slice: x: 4, y: 4, z: 4, core: 2. Of those that a mesh axis runs over, the one named last changes fastest.
Arguments:
- app_rhs: float32 [98304, 128], P(('leaf', 'front')), may hold values from -6 to 6
- pivot_source: int32 [98304], P(('leaf', 'front')), may hold values from 0 to 98303, as said below
- row_owner: int32 [98304], P(('leaf', 'front')), may hold values from 0 to 98303, as said below
- leaf_inverse: float32 [16, 8, 384, 3072], P('leaf', 'front'), may hold values from -1 to 2, as said below
- leaf_coupling: float32 [16, 8, 384, 2048], P('leaf', 'front'), may hold values from -0.054126587 to 0.054126587
- sep1_inverse: float32 [16, 8, 128, 2048], P('leaf', 'front'), may hold values from -1 to 2, as said below
- sep1_coupling: float32 [16, 8, 128, 4096], P('leaf', 'front'), may hold values from -0.06629126 to 0.06629126
- sep2_inverse: float32 [16, 8, 128, 4096], P('leaf', 'front'), may hold values from -1 to 2, as said below
- sep2_coupling: float32 [16, 8, 128, 8192], P('leaf', 'front'), may hold values from -0.046875 to 0.046875
- sep3_inverse: float32 [16, 8, 128, 8192], P('leaf', 'front'), may hold values from -1 to 2, as said below
Outputs:
- solution: float32 [98304, 128], P(('leaf', 'front'))
Inputs may be any that keep to these rules, and one draw needn't show every extreme that they name: `pivot_source`: A permutation. Row e of pivot_rhs comes from a device's block of 768 application rows; one block's rows go to at most 64 blocks of pivot rows, at most 15 rows from one block to one block, and some pair of blocks carries exactly 15 rows. The inverse of pivot_source: pivot_source[row_owner[i]] = i. `leaf_inverse`: each front's matrix is the identity plus dense entries of magnitude at most 2 / sqrt of the front's pivot rows. `sep1_inverse`: as leaf_inverse. `sep2_inverse`: as leaf_inverse. `sep3_inverse`: as leaf_inverse.
All inputs are finite; a program needn't handle non-finite values.
Results may differ from a plain program's by a relative error of at most 0.00011.
Values sent between devices are 32-bit elements; how exact they have to be, the bound alone decides.
No kernel may reach another device: no remote copies, remote signals or barrier semaphores. Data moves between devices by JAX's collectives and lax.ppermute only.
A program may use at most 128 MiB of HBM per device.

v0:
```python
import jax
import jax.numpy as jnp
from jax import lax
from jax.experimental import pallas as pl
from jax.experimental.pallas import tpu as pltpu
from jax.sharding import PartitionSpec as P


LEAF_PIV = 384
SEP_PIV = 128
PIVOTS = (LEAF_PIV, SEP_PIV, SEP_PIV, SEP_PIV)
AXES = ("leaf", "front")
F32 = jnp.float32
BF16 = jnp.bfloat16
SLOTS = 16
CHIPS = 4
CORE = 1
PLANE = 32
VMEM = pltpu.VMEM
HBM = pltpu.HBM


def params(mib):
    return pltpu.CompilerParams(vmem_limit_bytes=mib * 2**20)


def on_chip(x):
    return pltpu.with_memory_space_constraint(x, VMEM)


def off_chip(x):
    return pltpu.with_memory_space_constraint(x, HBM)


def vmem_specs(count):
    return [pl.BlockSpec(memory_space=VMEM)] * count


def call(body, outs, *args):
    return pl.pallas_call(
        body,
        in_specs=vmem_specs(len(args)),
        out_specs=vmem_specs(len(outs)),
        out_shape=[VMEM(shape, F32) for shape in outs],
        compiler_params=params(16),
    )(*[on_chip(a) for a in args])


def same_core_groups(height):
    leaves, fronts = lax.axis_size("leaf"), lax.axis_size("front")
    span = 2**height
    return [
        [(base + leaf) * fronts + 2 * chip + core for chip in range(fronts // 2) for leaf in range(span)]
        for base in range(0, leaves, span)
        for core in range(2)
    ]


def exchange(tiles, height):
    return lax.all_to_all(
        tiles, AXES, 0, 0, axis_index_groups=same_core_groups(min(height, 2)), tiled=True
    )


def swap(block, mask):
    count = lax.axis_size("leaf") * lax.axis_size("front")
    return lax.ppermute(block, AXES, [(i, i ^ mask) for i in range(count)])


def pair_of(x):
    high = x.astype(BF16)
    return high, (x - high.astype(F32)).astype(BF16)


def dot(a, b):
    return jnp.dot(a, b, preferred_element_type=F32)


def send_body(pieces, at_ref, *refs):
    count = len(pieces)
    sources = refs[: pieces[-1][0] + 1]
    sends = refs[len(sources) : len(sources) + count]
    stages = refs[len(sources) + count : len(sources) + 2 * count]
    in_sem, out_sem = refs[-2:]
    inward, outward = [], []
    for number, (source, cuts, place) in enumerate(pieces):
        width = stages[number].shape[1] // CHIPS
        inward.append([])
        for chip in range(CHIPS):
            block = 2 * cuts * chip + at_ref[place]
            here = pl.ds(pl.multiple_of(block * width, 128), width)
            inward[-1].append(
                pltpu.make_async_copy(
                    sources[source].at[:, here],
                    stages[number].at[:, pl.ds(chip * width, width)],
                    in_sem.at[number * CHIPS + chip],
                )
            )
        outward.append(pltpu.make_async_copy(stages[number], sends[number], out_sem.at[number]))
    for group in inward:
        for copy in group:
            copy.start()
    for group, after in zip(inward, outward):
        for copy in group:
            copy.wait()
        after.start()
    for copy in outward:
        copy.wait()


def cut_sends(places, matrices, pieces):
    shapes = [(matrices[m].shape[0], matrices[m].shape[1] // (2 * cuts)) for m, cuts, _ in pieces]
    return pl.pallas_call(
        lambda *refs: send_body(pieces, *refs),
        in_specs=[pl.BlockSpec(memory_space=pltpu.SMEM)]
        + [pl.BlockSpec(memory_space=HBM)] * len(matrices),
        out_specs=[pl.BlockSpec(memory_space=HBM)] * len(pieces),
        out_shape=[HBM(shape, F32) for shape in shapes],
        scratch_shapes=[VMEM(shape, F32) for shape in shapes]
        + [
            pltpu.SemaphoreType.DMA((CHIPS * len(pieces),)),
            pltpu.SemaphoreType.DMA((len(pieces),)),
        ],
        compiler_params=params(20),
    )(places, *[off_chip(m) for m in matrices])


def stepped(body, outs, places, mats, *args, scratch=()):
    matrix, others = mats[0], mats[1:]
    rows, width = others[0].shape[0], others[0].shape[1] // CHIPS
    cuts = matrix.shape[1] // (2 * CHIPS * width)
    own = pl.BlockSpec((rows, width), lambda step, at: (0, 2 * cuts * step + at[cuts - 1]))
    rest = pl.BlockSpec((rows, width), lambda step, at: (0, step))
    return pl.pallas_call(
        body,
        grid_spec=pltpu.PrefetchScalarGridSpec(
            num_scalar_prefetch=1,
            grid=(CHIPS,),
            in_specs=[own] + [rest] * len(others) + vmem_specs(len(args)),
            out_specs=vmem_specs(len(outs)),
            scratch_shapes=list(scratch),
        ),
        out_shape=[VMEM(shape, F32) for shape in outs],
        compiler_params=params(16),
    )(places, off_chip(matrix), *[off_chip(m) for m in others], *[on_chip(a) for a in args])


def apply_body(at_ref, *refs):
    blocks, (vec_ref, out_ref, acc_ref) = refs[:-3], refs[-3:]
    rows, width = blocks[0].shape
    total_rows, count = len(blocks) * rows, vec_ref.shape[1]
    step = pl.program_id(0)
    at = pl.ds(pl.multiple_of(step * width, 128), width)
    left = pair_of(jnp.concatenate([b[...] for b in blocks], axis=0))
    right = pair_of(vec_ref[at, :])
    full = dot(jnp.concatenate(left, axis=0), jnp.concatenate(right, axis=1))
    total = full[:total_rows, :count] + full[:total_rows, count:]
    total += full[total_rows:, :count] + full[total_rows:, count:]

    @pl.when(step == 0)
    def _():
        acc_ref[...] = total

    @pl.when(step > 0)
    def _():
        acc_ref[...] += total

    @pl.when(step == CHIPS - 1)
    def _():
        for part in range(len(blocks)):
            out_ref[part] = acc_ref[part * rows : (part + 1) * rows]


def applied(places, mats, vectors):
    rows, count = mats[0].shape[0], vectors.shape[1]
    shape = (len(mats), rows, count)
    acc = VMEM((len(mats) * rows, count), F32)
    (out,) = stepped(apply_body, [shape], places, mats, vectors, scratch=[acc])
    return out


def spread(blocks, vector, out_ref):
    high, low = pair_of(vector.T)
    left = jnp.concatenate([high, low], axis=0)
    count, width = vector.shape[1], blocks[0].shape[1]
    at = pl.ds(pl.multiple_of(pl.program_id(0) * width, 128), width)
    up, down = pair_of(jnp.concatenate([b[...] for b in blocks], axis=0))
    full = dot(left, up) + dot(left, down)
    out_ref[at, :] = (full[:count] + full[count:]).T


def rows_of(*tiles):
    return jnp.concatenate(tiles, axis=0)


def joined(here_ref, there_ref):
    return rows_of(here_ref[0] + there_ref[1], here_ref[1] + there_ref[0])


def forward_body(at_ref, *refs):
    blocks, (here_ref, there_ref, out_ref, solved_ref) = refs[:-4], refs[-4:]
    solved = joined(here_ref, there_ref)
    solved_ref[...] = solved
    spread(blocks, solved, out_ref)


def plane_body(at_ref, *refs):
    blocks, (solved_ref, far_ref, out_ref) = refs[:-3], refs[-3:]
    spread(blocks, rows_of(solved_ref[...], far_ref[...]), out_ref)


def top_body(at_ref, *refs):
    blocks, (here_ref, there_ref, out_ref) = refs[:-3], refs[-3:]
    vector = rows_of(*[here_ref[part] + there_ref[part ^ 2] for part in range(4)])
    spread(blocks, vector, out_ref)


def backward_body(at_ref, *refs):
    blocks, (here_ref, there_ref, solved_ref, out_ref) = refs[:-4], refs[-4:]
    spread(blocks, solved_ref[...] - joined(here_ref, there_ref), out_ref)


def joined_body(here_ref, there_ref, out_ref):
    out_ref[...] = joined(here_ref, there_ref)


def core_pair_body(here_ref, there_ref, out_ref):
    for part in range(4):
        out_ref[part] = here_ref[part] + there_ref[part ^ 1]


def plane_pair_body(here_ref, there_ref, out_ref):
    for part in range(2):
        out_ref[part] = here_ref[part] + there_ref[part]


def minus_sum_body(tiles_ref, base_ref, out_ref):
    share = base_ref[...] - jnp.sum(tiles_ref[...], axis=0)
    out_ref[...] = jnp.broadcast_to(share[None], out_ref.shape)


def sum_body(tiles_ref, share_ref, out_ref):
    share = jnp.sum(tiles_ref[...], axis=0)
    share_ref[...] = share
    out_ref[...] = jnp.broadcast_to(share[None], out_ref.shape)


def slots_body(index_ref, rows_ref, out_ref):
    rows = rows_ref[...]
    width = rows.shape[1]
    high, middle = pair_of(rows)
    low = (rows - high.astype(F32) - middle.astype(F32)).astype(BF16)
    parts = jnp.concatenate([high, middle, low], axis=1)
    index = index_ref[...]

    @pl.loop(0, out_ref.shape[0] // 256)
    def _(step):
        start = pl.multiple_of(step * 256, 256)
        slot = lax.broadcasted_iota(jnp.int32, (256, rows.shape[0]), 0) + start
        chosen = dot((slot == index).astype(F32).astype(BF16), parts)
        out_ref[pl.ds(start, 256), :] = (
            chosen[:, :width] + chosen[:, width : 2 * width] + chosen[:, 2 * width :]
        )


def to_slots(index, rows):
    peers = lax.axis_size("leaf") * lax.axis_size("front")
    return pl.pallas_call(
        slots_body,
        in_specs=vmem_specs(2),
        out_specs=pl.BlockSpec(memory_space=VMEM),
        out_shape=VMEM((peers * SLOTS, rows.shape[1]), F32),
        compiler_params=params(16),
    )(index[None, :], rows)


def rank_among(keys, order):
    same = (keys[:, None] == keys[None, :]) & (order[None, :] < order[:, None])
    return jnp.sum(same.astype(jnp.int32), axis=1)


def move_rows(outgoing):
    tiles = outgoing.reshape(-1, SLOTS, outgoing.shape[1])
    return lax.all_to_all(tiles, AXES, 0, 0, tiled=True).reshape(outgoing.shape)


def whole_solve(app_rhs, pivot_source, row_owner, *matrices):
    core = lax.axis_index("front") % 2
    plane = lax.axis_index("leaf") // 4 % 2
    row_count, width = app_rhs.shape
    matrices = [m[0, 0] for m in matrices]

    destination = row_owner // row_count
    send_index = destination * SLOTS + rank_among(
        destination, jnp.arange(row_count, dtype=jnp.int32)
    )
    anchor = pivot_source // row_count
    recv_index = anchor * SLOTS + rank_among(anchor, pivot_source)
    outgoing = to_slots(send_index, app_rhs)

    def all_places(core, plane):
        near, far = 2 * core + plane, 2 * (1 - core) + plane
        table = [core, near, 1 - core, far, near + 1 - 2 * plane, far + 1 - 2 * plane]
        return jnp.stack(table).astype(jnp.int32)

    places = all_places(core, plane)
    sends = cut_sends(places, matrices[:2], [(0, 1, 2), (1, 1, 2)])
    mats = [[matrices[m], swap(sends[m], CORE)] for m in range(2)]
    ordered = move_rows(outgoing)[recv_index]
    ordered, core, plane = lax.optimization_barrier((ordered, core, plane))
    late = [(m, 1, 2) for m in range(3)] + [(m, 2, p) for m in (3, 4) for p in (3, 4, 5)]
    sends = cut_sends(all_places(core, plane), matrices[2:], late)
    mats += [[matrices[m], swap(sends[m - 2], CORE)] for m in range(2, 5)]
    mats += [[matrices[m], swap(sends[3 * m - 12], CORE)] for m in (5, 6)]
    for number, piece in enumerate((4, 5, 7, 8)):
        half = swap(sends[piece], (PLANE, PLANE | CORE)[number % 2])
        mats[5 + number // 2].append(half)
    inverses = (mats[0], mats[2], mats[4], mats[6])
    couplings = (mats[1], mats[3], mats[5])

    starts = (0, LEAF_PIV, LEAF_PIV + SEP_PIV, LEAF_PIV + 2 * SEP_PIV)
    sizes = (CHIPS, 2 * CHIPS, 4 * CHIPS, 4 * CHIPS)
    own = [ordered[at : at + rows] for at, rows in zip(starts, PIVOTS)]
    tiles = jnp.broadcast_to(own[0][None], (sizes[0], LEAF_PIV, width))
    solved = []
    for height in range(3):
        gathered = exchange(tiles, height).reshape(-1, width)
        here = applied(places, inverses[height], gathered)
        there = swap(here, CORE)
        outs = [(couplings[height][1].shape[1], width), (2 * PIVOTS[height], width)]
        if height < 2:
            carried, forward = stepped(
                forward_body, outs, places, couplings[height], here, there
            )
        else:
            (forward,) = call(joined_body, outs[1:], here, there)
            far_rows = swap(forward, PLANE)
            (carried,) = stepped(
                plane_body, outs[:1], places, couplings[height], forward, far_rows
            )
        solved.append(forward)
        arrived = exchange(carried.reshape(-1, SEP_PIV, width), height + 1)
        (tiles,) = call(
            minus_sum_body, [(sizes[height + 1], SEP_PIV, width)], arrived, own[height + 1]
        )
    here = applied(places, inverses[3], exchange(tiles, 3).reshape(-1, width))
    (here,) = call(core_pair_body, [here.shape], here, swap(here, CORE))
    (spread_out,) = stepped(
        top_body, [(inverses[3][1].shape[1], width)], places, inverses[3], here, swap(here, PLANE)
    )
    pieces = [None, None, None, None]
    for height in (3, 2, 1):
        arrived = exchange(spread_out.reshape(-1, SEP_PIV, width), height)
        pieces[height], tiles = call(
            sum_body, [(SEP_PIV, width), (sizes[height], SEP_PIV, width)], arrived
        )
        here = applied(places, couplings[height - 1], exchange(tiles, height).reshape(-1, width))
        if height == 3:
            (here,) = call(plane_pair_body, [(2, SEP_PIV, width)], here, swap(here[2:], PLANE))
        there = swap(here, CORE)
        mats_low = inverses[height - 1]
        outs = [(mats_low[1].shape[1], width)]
        (spread_out,) = stepped(
            backward_body, outs, places, mats_low, here, there, solved[height - 1]
        )
    pieces[0] = exchange(spread_out.reshape(-1, LEAF_PIV, width), 0).sum(axis=0)
    pivot_order = jnp.concatenate(pieces, axis=0)
    return move_rows(to_slots(recv_index, pivot_order))[send_index]


def solution(mesh):
    wide = P("leaf", "front", None, None)
    in_specs = (P(AXES, None), P(AXES), P(AXES)) + (wide,) * 7
    return jax.shard_map(
        whole_solve, mesh=mesh, in_specs=in_specs, out_specs=P(AXES, None), check_vma=False
    )
```

profile of v0, /device:TPU:1, one launch (start us, length us, event | category | flops | bytes accessed | tf_op | source)
XLA Modules:
  0.0 455.1 jit_solution(13445045895152429447)
XLA Ops:
  0.1 4.2 shard_map.100
  4.3 1.5 collective-permute-start
  6.2 4.0 shard_map.101
  10.2 10.2 %all-to-all-start = ((f32[128,16,128]{2,1,0:T(8,128)}), f32[128,16,128]{2,1,0:T(8,128)S(1)}, u32[]{:S(2)}, u32[]{:S(2)}) async-start(f32[128,16,128]{2,1,0:T(8,128)} %bitcast.9), calls=%async_computation | async-start | bytes 2097152 | tf_op jit(solution)/shard_map/all_to_all | solution.py:284
  22.1 17.5 %all-to-all-done = f32[128,16,128]{2,1,0:T(8,128)S(1)} async-done(((f32[128,16,128]{2,1,0:T(8,128)}), f32[128,16,128]{2,1,0:T(8,128)S(1)}, u32[]{:S(2)}, u32[]{:S(2)}) %all-to-all-start) | async-done | bytes 1048608 | tf_op jit(solution)/shard_map/all_to_all | solution.py:284
  39.6 1.6 gather_fusion
  41.3 13.8 %all_to_all.80 = f32[4,384,128]{2,1,0:T(8,128)S(1)} all-to-all(f32[4,384,128]{2,1,0:T(8,128)S(1)} %broadcast_in_dim.13), channel_id=1, replica_groups={{0,2,4,6},{1,3,5,7},{8,10,12,14},{9,11,13,15},{16,18,20,22},{17,19,21,2..., dimensions={0} | all-to-all | bytes 1572864 | tf_op jit(solution)/shard_map/all_to_all | solution.py:60
  55.1 5.1 %shard_map.103.refs_2_ = f32[2,384,128]{2,1,0:T(8,128)S(1)} custom-call(s32[6]{0:T(128)S(1)} %stack.48.refs_0_.at_ref, f32[384,3072]{1,0:T(8,128)} %bitcast.48, f32[384,1536]{1,0:T(8,128)} %collective-permute-done.refs_1_, f32[1536,128]{1,0:T(8,128)S(1)} %bitcast.43), custom_call_target="tpu_custom_call" | custom-call | tf_op jit(solution)/shard_map/pallas_call | solution.py:134
  60.2 1.9 collective-permute-start.11
  62.2 1.3 collective-permute-done.11.refs_3_
  63.4 5.2 %shard_map.104 = (f32[1024,128]{1,0:T(8,128)}, f32[768,128]{1,0:T(8,128)S(1)}) custom-call(s32[6]{0:T(128)S(1)} %stack.48.refs_0_.at_ref, f32[384,2048]{1,0:T(8,128)} %bitcast.57, f32[384,1024]{1,0:T(8,128)} %copy-done.1, f32[2,384,128]{2,1,0:T(8,128)S(1)} %shard_map.103.refs_2_, f32[2,384,128]{2,1,0:T(8,128)S(1)} %collective-permute-done.11.refs_3_), custom_call_target="tpu_custom_call" | custom-call | tf_op jit(solution)/shard_map/pallas_call | solution.py:134
  68.6 3.5 all-to-all-start.2
  72.2 7.7 %shard_map.102 = (f32[128,1024]{1,0:T(8,128)}, f32[128,2048]{1,0:T(8,128)}, f32[128,2048]{1,0:T(8,128)}, f32[128,2048]{1,0:T(8,128)}, f32[128,2048]{1,0:T(8,128)...) custom-call(s32[6]{0:T(128)S(1)} %stack.55.refs_0_, ...), custom_call_target="tpu_custom_call" | custom-call | tf_op jit(solution)/shard_map/pallas_call | solution.py:113
  82.1 4.5 all-to-all-start.3
  86.6 9.2 %all-to-all-done.3 = f32[8,128,128]{2,1,0:T(8,128)S(1)} async-done(((f32[8,128,128]{2,1,0:T(8,128)}), f32[8,128,128]{2,1,0:T(8,128)S(1)}, u32[]{:S(2)}, u32[]{:S(2)}) %all-to-all-start.3) | async-done | bytes 524320 | tf_op jit(solution)/shard_map/all_to_all | solution.py:60
  95.8 3.3 shard_map.106.refs_2_
  99.2 1.3 collective-permute-start.12
  101.5 5.0 %shard_map.107 = (f32[2048,128]{1,0:T(8,128)}, f32[256,128]{1,0:T(8,128)S(1)}) custom-call(s32[6]{0:T(128)S(1)} %stack.48.refs_0_.at_ref, f32[128,4096]{1,0:T(8,128)} %bitcast.63, f32[128,2048]{1,0:T(8,128)} %copy-done.4, f32[2,128,128]{2,1,0:T(8,128)S(1)} %shard_map.106.refs_2_, f32[2,128,128]{2,1,0:T(8,128)S(1)} %collective-permute-done.12.refs_3_), custom_call_target="tpu_custom_call" | custom-call | tf_op jit(solution)/shard_map/pallas_call | solution.py:134
  106.5 3.7 all-to-all-start.4
  110.6 16.4 %all-to-all-done.4.tiles_ref = f32[16,128,128]{2,1,0:T(8,128)S(1)} async-done(((f32[16,128,128]{2,1,0:T(8,128)}), f32[16,128,128]{2,1,0:T(8,128)S(1)}, u32[]{:S(2)}, u32[]{:S(2)}) %all-to-all-start.4) | async-done | bytes 1048608 | tf_op jit(solution)/shard_map/all_to_all | solution.py:60
  128.1 3.8 all-to-all-start.5
  131.8 1.9 collective-permute-start.5
  133.7 1.7 collective-permute-start.7
  135.5 11.6 %all-to-all-done.5 = f32[16,128,128]{2,1,0:T(8,128)S(1)} async-done(((f32[16,128,128]{2,1,0:T(8,128)}), f32[16,128,128]{2,1,0:T(8,128)S(1)}, u32[]{:S(2)}, u32[]{:S(2)}) %all-to-all-start.5) | async-done | bytes 1048608 | tf_op jit(solution)/shard_map/all_to_all | solution.py:60
  147.1 3.7 shard_map.109.here_ref
  150.8 3.1 collective-permute-start.13
  155.0 3.7 collective-permute-done.6.refs_2_
  158.7 23.3 %collective-permute-done.7.refs_3_ = f32[128,2048]{1,0:T(8,128)} collective-permute-done((f32[128,2048]{1,0:T(8,128)}, f32[128,2048]{1,0:T(8,128)}, u32[]{:S(2)}, u32[]{:S(2)}) %collective-permute-start.7) | collective-permute-done | bytes 1048608 | tf_op jit(solution)/shard_map/ppermute | solution.py:67
  182.0 1.9 collective-permute-done.14.refs_5_
  183.9 5.8 %shard_map.111 = f32[2048,128]{1,0:T(8,128)} custom-call(s32[6]{0:T(128)S(1)} %stack.48.refs_0_.at_ref, f32[128,8192]{1,0:T(8,128)} %bitcast.54, f32[128,2048]{1,0:T(8,128)} %collective-permute-done.5.refs_1_, f32[128,2048]{1,0:T(8,128)} %collective-permute-done.6.refs_2_, f32[128,2048]{1,0:T(8,128)} %collective-permute-done.7.refs_3_, ...), custom_call_target="tpu_custom_call" | custom-call | tf_op jit(solution)/shard_map/pallas_call | solution.py:134
  189.7 6.8 %all-to-all-start.6 = ((f32[16,128,128]{2,1,0:T(8,128)}), f32[16,128,128]{2,1,0:T(8,128)S(1)}, u32[]{:S(2)}, u32[]{:S(2)}) async-start(f32[16,128,128]{2,1,0:T(8,128)} %bitcast.26), calls=%async_computation.6 | async-start | bytes 2097152 | tf_op jit(solution)/shard_map/all_to_all | solution.py:60
  196.5 1.3 collective-permute-start.8
  197.8 1.7 collective-permute-start.10
  199.5 12.4 %all-to-all-done.6.tiles_ref = f32[16,128,128]{2,1,0:T(8,128)S(1)} async-done(((f32[16,128,128]{2,1,0:T(8,128)}), f32[16,128,128]{2,1,0:T(8,128)S(1)}, u32[]{:S(2)}, u32[]{:S(2)}) %all-to-all-start.6) | async-done | bytes 1048608 | tf_op jit(solution)/shard_map/all_to_all | solution.py:60
  213.0 3.8 all-to-all-start.7
  216.8 5.9 %collective-permute-done.9.refs_2_ = f32[128,2048]{1,0:T(8,128)} collective-permute-done((f32[128,2048]{1,0:T(8,128)}, f32[128,2048]{1,0:T(8,128)}, u32[]{:S(2)}, u32[]{:S(2)}) %collective-permute-start.9) | collective-permute-done | bytes 1048608 | tf_op jit(solution)/shard_map/ppermute | solution.py:67
  222.7 22.7 %collective-permute-done.10.refs_3_ = f32[128,2048]{1,0:T(8,128)} collective-permute-done((f32[128,2048]{1,0:T(8,128)}, f32[128,2048]{1,0:T(8,128)}, u32[]{:S(2)}, u32[]{:S(2)}) %collective-permute-start.10) | collective-permute-done | bytes 1048608 | tf_op jit(solution)/shard_map/ppermute | solution.py:67
  245.4 4.5 shard_map.113.here_ref
  250.2 1.4 collective-permute-done.15.there_ref
  251.9 7.7 %collective-permute-done.16.refs_5_ = f32[4,128,128]{2,1,0:T(8,128)S(1)} collective-permute-done((f32[4,128,128]{2,1,0:T(8,128)S(1)}, f32[4,128,128]{2,1,0:T(8,128)S(1)}, u32[]{:S(2)}, u32[]{:S(2)}) %collective-permute-start.16) | collective-permute-done | bytes 262176 | tf_op jit(solution)/shard_map/ppermute | solution.py:67
  259.6 4.9 %shard_map.115 = f32[2048,128]{1,0:T(8,128)S(1)} custom-call(s32[6]{0:T(128)S(1)} %stack.48.refs_0_.at_ref, f32[128,8192]{1,0:T(8,128)} %bitcast.52, f32[128,2048]{1,0:T(8,128)} %copy-done.3, f32[128,2048]{1,0:T(8,128)} %collective-permute-done.9.refs_2_, f32[128,2048]{1,0:T(8,128)} %collective-permute-done.10.refs_3_, ...), custom_call_target="tpu_custom_call" | custom-call | tf_op jit(solution)/shard_map/pallas_call | solution.py:134
  264.4 22.2 %all_to_all.81.tiles_ref = f32[16,128,128]{2,1,0:T(8,128)S(1)} all-to-all(f32[16,128,128]{2,1,0:T(8,128)S(1)} %bitcast.39), channel_id=1, replica_groups={{0,8,16,24,2,10,18,26,4,12,20,28,6,14,22,30},{1,9,17,25,3,11,19,27,5,13..., dimensions={0} | all-to-all | bytes 2097152 | tf_op jit(solution)/shard_map/all_to_all | solution.py:60
  286.8 18.4 %all_to_all.82 = f32[16,128,128]{2,1,0:T(8,128)S(1)} all-to-all(f32[16,128,128]{2,1,0:T(8,128)S(1)} %get-tuple-element.45), channel_id=1, replica_groups={{0,8,16,24,2,10,18,26,4,12,20,28,6,14,22,30},{1,9,17,25,3,11,19,27,5,13..., dimensions={0} | all-to-all | bytes 2097152 | tf_op jit(solution)/shard_map/all_to_all | solution.py:60
  305.2 4.5 shard_map.117.here_ref
  309.8 3.8 collective-permute-done.17.there_ref
  313.6 4.3 collective-permute-start.18
  318.9 4.1 shard_map.119
  323.0 19.1 %all_to_all.83.tiles_ref = f32[16,128,128]{2,1,0:T(8,128)S(1)} all-to-all(f32[16,128,128]{2,1,0:T(8,128)S(1)} %bitcast.41), channel_id=1, replica_groups={{0,8,16,24,2,10,18,26,4,12,20,28,6,14,22,30},{1,9,17,25,3,11,19,27,5,13..., dimensions={0} | all-to-all | bytes 2097152 | tf_op jit(solution)/shard_map/all_to_all | solution.py:60
  342.2 18.3 %all_to_all.84 = f32[16,128,128]{2,1,0:T(8,128)S(1)} all-to-all(f32[16,128,128]{2,1,0:T(8,128)S(1)} %get-tuple-element.46), channel_id=1, replica_groups={{0,8,16,24,2,10,18,26,4,12,20,28,6,14,22,30},{1,9,17,25,3,11,19,27,5,13..., dimensions={0} | all-to-all | bytes 2097152 | tf_op jit(solution)/shard_map/all_to_all | solution.py:60
  360.5 3.7 shard_map.121.refs_2_
  364.2 3.3 collective-permute-start.19
  368.5 3.6 shard_map.122
  372.2 11.7 %all_to_all.85.tiles_ref = f32[8,128,128]{2,1,0:T(8,128)S(1)} all-to-all(f32[8,128,128]{2,1,0:T(8,128)S(1)} %bitcast.46), channel_id=1, replica_groups={{0,8,2,10,4,12,6,14},{1,9,3,11,5,13,7,15},{16,24,18,26,20,28,22,30},{17..., dimensions={0} | all-to-all | bytes 1048576 | tf_op jit(solution)/shard_map/all_to_all | solution.py:60
  383.9 11.0 %all_to_all.86 = f32[8,128,128]{2,1,0:T(8,128)S(1)} all-to-all(f32[8,128,128]{2,1,0:T(8,128)S(1)} %get-tuple-element.48), channel_id=1, replica_groups={{0,8,2,10,4,12,6,14},{1,9,3,11,5,13,7,15},{16,24,18,26,20,28,22,30},{17..., dimensions={0} | all-to-all | bytes 1048576 | tf_op jit(solution)/shard_map/all_to_all | solution.py:60
  394.9 4.2 shard_map.124.refs_2_
  399.1 2.5 collective-permute-start.20
  401.6 1.3 collective-permute-done.20.refs_3_
  402.9 6.3 %shard_map.125 = f32[1536,128]{1,0:T(8,128)} custom-call(s32[6]{0:T(128)S(1)} %stack.48.refs_0_.at_ref, f32[384,3072]{1,0:T(8,128)} %bitcast.49, f32[384,1536]{1,0:T(8,128)} %collective-permute-done.refs_1_, f32[2,384,128]{2,1,0:T(8,128)S(1)} %shard_map.124.refs_2_, f32[2,384,128]{2,1,0:T(8,128)S(1)} %collective-permute-done.20.refs_3_, ...), custom_call_target="tpu_custom_call" | custom-call | tf_op jit(solution)/shard_map/pallas_call | solution.py:134
  409.2 3.5 all-to-all-start.14
  412.7 12.0 %all-to-all-done.14 = f32[4,384,128]{2,1,0:T(8,128)S(1)} async-done(((f32[4,384,128]{2,1,0:T(8,128)}), f32[4,384,128]{2,1,0:T(8,128)S(1)}, u32[]{:S(2)}, u32[]{:S(2)}) %all-to-all-start.14) | async-done | bytes 786464 | tf_op jit(solution)/shard_map/all_to_all | solution.py:60
  424.8 4.0 shard_map.126
  428.7 4.7 %all-to-all-start.15 = ((f32[128,16,128]{2,1,0:T(8,128)}), f32[128,16,128]{2,1,0:T(8,128)S(1)}, u32[]{:S(2)}, u32[]{:S(2)}) async-start(f32[128,16,128]{2,1,0:T(8,128)} %bitcast.35), calls=%async_computation.15 | async-start | bytes 2097152 | tf_op jit(solution)/shard_map/all_to_all | solution.py:284
  433.5 19.3 %all-to-all-done.15 = f32[128,16,128]{2,1,0:T(8,128)S(1)} async-done(((f32[128,16,128]{2,1,0:T(8,128)}), f32[128,16,128]{2,1,0:T(8,128)S(1)}, u32[]{:S(2)}, u32[]{:S(2)}) %all-to-all-start.15) | async-done | bytes 1048608 | tf_op jit(solution)/shard_map/all_to_all | solution.py:284
  452.8 2.3 gather_fusion.1
  (70 shorter events, 12.4 us)
Async XLA Ops:
  0.1 5.7 %copy-start.9 = (s32[768]{0:T(1024)S(1)}, s32[768]{0:T(1024)}, u32[]{:S(2)}) copy-start(s32[768]{0:T(1024)} %param.12) | copy-start | bytes 9220
  0.1 6.1 %copy-start = (f32[768,128]{1,0:T(8,128)S(1)}, f32[768,128]{1,0:T(8,128)}, u32[]{:S(2)}) copy-start(f32[768,128]{1,0:T(8,128)} %rows_ref.1) | copy-start | bytes 1179652
  4.3 17.3 %copy-start.8 = (s32[768]{0:T(1024)S(1)}, s32[768]{0:T(1024)}, u32[]{:S(2)}) copy-start(s32[768]{0:T(1024)} %param.11) | copy-start | bytes 9220
  4.3 50.8 %collective-permute-start = (f32[384,1536]{1,0:T(8,128)}, f32[384,1536]{1,0:T(8,128)}, u32[]{:S(2)}, u32[]{:S(2)}) collective-permute-start(f32[384,1536]{1,0:T(8,128)} %get-tuple-element.29), channel_id=1, source_target_pairs={{0,1},{1,0},{2,3},{3,2},{4,5},{5,4},{6,7},{7,6},{8,9},{9,8},{10,11... | collective-permute-start | bytes 7077896 | tf_op jit(solution)/shard_map/ppermute | solution.py:67
  10.2 29.5 %all-to-all-start = ((f32[128,16,128]{2,1,0:T(8,128)}), f32[128,16,128]{2,1,0:T(8,128)S(1)}, u32[]{:S(2)}, u32[]{:S(2)}) async-start(f32[128,16,128]{2,1,0:T(8,128)} %bitcast.9), calls=%async_computation | async-start | bytes 2097152 | tf_op jit(solution)/shard_map/all_to_all | solution.py:284
  20.4 41.8 %collective-permute-start.1 = (f32[384,1024]{1,0:T(8,128)}, f32[384,1024]{1,0:T(8,128)S(1)}, u32[]{:S(2)}, u32[]{:S(2)}) collective-permute-start(f32[384,1024]{1,0:T(8,128)} %get-tuple-element.30), channel_id=1, source_target_pairs={{0,1},{1,0},{2,3},{3,2},{4,5},{5,4},{6,7},{7,6},{8,9},{9,8},{10,11... | collective-permute-start | bytes 4718600 | tf_op jit(solution)/shard_map/ppermute | solution.py:67
  41.2 19.0 %copy-start.6 = (f32[768,128]{1,0:T(8,128)}, f32[768,128]{1,0:T(8,128)S(1)}, u32[]{:S(2)}) copy-start(f32[768,128]{1,0:T(8,128)S(1)} %gather_fusion) | copy-start | bytes 1179652
  60.2 3.2 collective-permute-start.11
  62.2 1.3 copy-start.1
  68.6 12.6 %all-to-all-start.2 = ((f32[8,128,128]{2,1,0:T(8,128)}), f32[8,128,128]{2,1,0:T(8,128)S(1)}, u32[]{:S(2)}, u32[]{:S(2)}) async-start(f32[8,128,128]{2,1,0:T(8,128)} %bitcast.22), calls=%async_computation.2 | async-start | bytes 1048576 | tf_op jit(solution)/shard_map/all_to_all | solution.py:60
  72.1 8.3 %copy-start.7 = (f32[768,128]{1,0:T(8,128)S(1)}, f32[768,128]{1,0:T(8,128)}, u32[]{:S(2)}) copy-start(f32[768,128]{1,0:T(8,128)} %copy-done.6) | copy-start | bytes 1179652
  79.9 20.6 %collective-permute-start.3 = (f32[128,2048]{1,0:T(8,128)}, f32[128,2048]{1,0:T(8,128)S(1)}, u32[]{:S(2)}, u32[]{:S(2)}) collective-permute-start(f32[128,2048]{1,0:T(8,128)} %get-tuple-element.34), channel_id=1, source_target_pairs={{0,1},{1,0},{2,3},{3,2},{4,5},{5,4},{6,7},{7,6},{8,9},{9,8},{10,11... | collective-permute-start | bytes 3145736 | tf_op jit(solution)/shard_map/ppermute | solution.py:67
  80.3 6.3 %collective-permute-start.2 = (f32[128,1024]{1,0:T(8,128)}, f32[128,1024]{1,0:T(8,128)S(1)}, u32[]{:S(2)}, u32[]{:S(2)}) collective-permute-start(f32[128,1024]{1,0:T(8,128)} %get-tuple-element.33), channel_id=1, source_target_pairs={{0,1},{1,0},{2,3},{3,2},{4,5},{5,4},{6,7},{7,6},{8,9},{9,8},{10,11... | collective-permute-start | bytes 1572872 | tf_op jit(solution)/shard_map/ppermute | solution.py:67
  82.1 13.7 %all-to-all-start.3 = ((f32[8,128,128]{2,1,0:T(8,128)}), f32[8,128,128]{2,1,0:T(8,128)S(1)}, u32[]{:S(2)}, u32[]{:S(2)}) async-start(f32[8,128,128]{2,1,0:T(8,128)} %shard_map.105), calls=%async_computation.3 | async-start | bytes 1048576 | tf_op jit(solution)/shard_map/all_to_all | solution.py:60
  86.6 9.2 %copy-start.5 = (f32[128,1024]{1,0:T(8,128)}, f32[128,1024]{1,0:T(8,128)S(1)}, u32[]{:S(2)}) copy-start(f32[128,1024]{1,0:T(8,128)S(1)} %collective-permute-done.2.refs_1_) | copy-start | bytes 1572868
  99.2 2.3 collective-permute-start.12
  100.5 1.0 copy-start.4
  106.5 20.4 %all-to-all-start.4 = ((f32[16,128,128]{2,1,0:T(8,128)}), f32[16,128,128]{2,1,0:T(8,128)S(1)}, u32[]{:S(2)}, u32[]{:S(2)}) async-start(f32[16,128,128]{2,1,0:T(8,128)} %bitcast.24), calls=%async_computation.4 | async-start | bytes 2097152 | tf_op jit(solution)/shard_map/all_to_all | solution.py:60
  110.2 25.3 %collective-permute-start.4 = (f32[128,2048]{1,0:T(8,128)}, f32[128,2048]{1,0:T(8,128)S(1)}, u32[]{:S(2)}, u32[]{:S(2)}) collective-permute-start(f32[128,2048]{1,0:T(8,128)} %get-tuple-element.35), channel_id=1, source_target_pairs={{0,1},{1,0},{2,3},{3,2},{4,5},{5,4},{6,7},{7,6},{8,9},{9,8},{10,11... | collective-permute-start | bytes 3145736 | tf_op jit(solution)/shard_map/ppermute | solution.py:67
  128.1 19.0 %all-to-all-start.5 = ((f32[16,128,128]{2,1,0:T(8,128)}), f32[16,128,128]{2,1,0:T(8,128)S(1)}, u32[]{:S(2)}, u32[]{:S(2)}) async-start(f32[16,128,128]{2,1,0:T(8,128)} %shard_map.108), calls=%async_computation.5 | async-start | bytes 2097152 | tf_op jit(solution)/shard_map/all_to_all | solution.py:60
  131.8 23.2 %collective-permute-start.5 = (f32[128,2048]{1,0:T(8,128)}, f32[128,2048]{1,0:T(8,128)}, u32[]{:S(2)}, u32[]{:S(2)}) collective-permute-start(f32[128,2048]{1,0:T(8,128)} %get-tuple-element.36), channel_id=1, source_target_pairs={{0,1},{1,0},{2,3},{3,2},{4,5},{5,4},{6,7},{7,6},{8,9},{9,8},{10,11... | collective-permute-start | bytes 3145736 | tf_op jit(solution)/shard_map/ppermute | solution.py:67
  133.7 24.9 %collective-permute-start.6 = (f32[128,2048]{1,0:T(8,128)}, f32[128,2048]{1,0:T(8,128)}, u32[]{:S(2)}, u32[]{:S(2)}) collective-permute-start(f32[128,2048]{1,0:T(8,128)} %get-tuple-element.37), channel_id=1, source_target_pairs={{0,32},{1,33},{2,34},{3,35},{4,36},{5,37},{6,38},{7,39},{8,40},{9,... | collective-permute-start | bytes 3145736 | tf_op jit(solution)/shard_map/ppermute | solution.py:67
  133.7 48.2 %collective-permute-start.7 = (f32[128,2048]{1,0:T(8,128)}, f32[128,2048]{1,0:T(8,128)}, u32[]{:S(2)}, u32[]{:S(2)}) collective-permute-start(f32[128,2048]{1,0:T(8,128)} %get-tuple-element.38), channel_id=1, source_target_pairs={{0,33},{1,32},{2,35},{3,34},{4,37},{5,36},{6,39},{7,38},{8,41},{9,... | collective-permute-start | bytes 3145736 | tf_op jit(solution)/shard_map/ppermute | solution.py:67
  135.5 11.6 %copy-start.2 = (f32[128,2048]{1,0:T(8,128)}, f32[128,2048]{1,0:T(8,128)S(1)}, u32[]{:S(2)}) copy-start(f32[128,2048]{1,0:T(8,128)S(1)} %collective-permute-done.4.refs_1_) | copy-start | bytes 3145732
  150.8 4.1 collective-permute-start.13
  154.9 29.0 %collective-permute-start.14 = (f32[256,128]{1,0:T(8,128)S(1)}, f32[256,128]{1,0:T(8,128)S(1)}, u32[]{:S(2)}, u32[]{:S(2)}) collective-permute-start(f32[256,128]{1,0:T(8,128)S(1)} %shard_map.110.refs_4_), channel_id=1, source_target_pairs={{0,32},{1,33},{2,34},{3,35},{4,36},{5,37},{6,38},{7,39},{8,40},{9,... | collective-permute-start | bytes 393224 | tf_op jit(solution)/shard_map/ppermute | solution.py:67
  189.7 22.3 %all-to-all-start.6 = ((f32[16,128,128]{2,1,0:T(8,128)}), f32[16,128,128]{2,1,0:T(8,128)S(1)}, u32[]{:S(2)}, u32[]{:S(2)}) async-start(f32[16,128,128]{2,1,0:T(8,128)} %bitcast.26), calls=%async_computation.6 | async-start | bytes 2097152 | tf_op jit(solution)/shard_map/all_to_all | solution.py:60
  196.5 20.4 %collective-permute-start.8 = (f32[128,2048]{1,0:T(8,128)}, f32[128,2048]{1,0:T(8,128)S(1)}, u32[]{:S(2)}, u32[]{:S(2)}) collective-permute-start(f32[128,2048]{1,0:T(8,128)} %get-tuple-element.39), channel_id=1, source_target_pairs={{0,1},{1,0},{2,3},{3,2},{4,5},{5,4},{6,7},{7,6},{8,9},{9,8},{10,11... | collective-permute-start | bytes 3145736 | tf_op jit(solution)/shard_map/ppermute | solution.py:67
  197.8 24.9 %collective-permute-start.9 = (f32[128,2048]{1,0:T(8,128)}, f32[128,2048]{1,0:T(8,128)}, u32[]{:S(2)}, u32[]{:S(2)}) collective-permute-start(f32[128,2048]{1,0:T(8,128)} %get-tuple-element.40), channel_id=1, source_target_pairs={{0,32},{1,33},{2,34},{3,35},{4,36},{5,37},{6,38},{7,39},{8,40},{9,... | collective-permute-start | bytes 3145736 | tf_op jit(solution)/shard_map/ppermute | solution.py:67
  197.8 47.7 %collective-permute-start.10 = (f32[128,2048]{1,0:T(8,128)}, f32[128,2048]{1,0:T(8,128)}, u32[]{:S(2)}, u32[]{:S(2)}) collective-permute-start(f32[128,2048]{1,0:T(8,128)} %get-tuple-element.41), channel_id=1, source_target_pairs={{0,33},{1,32},{2,35},{3,34},{4,37},{5,36},{6,39},{7,38},{8,41},{9,... | collective-permute-start | bytes 3145736 | tf_op jit(solution)/shard_map/ppermute | solution.py:67
  213.0 32.4 %all-to-all-start.7 = ((f32[16,128,128]{2,1,0:T(8,128)}), f32[16,128,128]{2,1,0:T(8,128)S(1)}, u32[]{:S(2)}, u32[]{:S(2)}) async-start(f32[16,128,128]{2,1,0:T(8,128)} %shard_map.112), calls=%async_computation.7 | async-start | bytes 2097152 | tf_op jit(solution)/shard_map/all_to_all | solution.py:60
  216.8 28.6 %copy-start.3 = (f32[128,2048]{1,0:T(8,128)}, f32[128,2048]{1,0:T(8,128)S(1)}, u32[]{:S(2)}) copy-start(f32[128,2048]{1,0:T(8,128)S(1)} %collective-permute-done.8.refs_1_) | copy-start | bytes 3145732
  249.9 1.6 collective-permute-start.15
  251.6 8.0 %collective-permute-start.16 = (f32[4,128,128]{2,1,0:T(8,128)S(1)}, f32[4,128,128]{2,1,0:T(8,128)S(1)}, u32[]{:S(2)}, u32[]{:S(2)}) collective-permute-start(f32[4,128,128]{2,1,0:T(8,128)S(1)} %shard_map.114.refs_4_), channel_id=1, source_target_pairs={{0,32},{1,33},{2,34},{3,35},{4,36},{5,37},{6,38},{7,39},{8,40},{9,... | collective-permute-start | bytes 786440 | tf_op jit(solution)/shard_map/ppermute | solution.py:67
  309.7 3.9 collective-permute-start.17
  313.6 5.3 %collective-permute-start.18 = (f32[2,128,128]{2,1,0:T(8,128)S(1)}, f32[2,128,128]{2,1,0:T(8,128)S(1)}, u32[]{:S(2)}, u32[]{:S(2)}) collective-permute-start(f32[2,128,128]{2,1,0:T(8,128)S(1)} %shard_map.118.refs_2_), channel_id=1, source_target_pairs={{0,1},{1,0},{2,3},{3,2},{4,5},{5,4},{6,7},{7,6},{8,9},{9,8},{10,11... | collective-permute-start | bytes 393224 | tf_op jit(solution)/shard_map/ppermute | solution.py:67
  364.2 4.3 collective-permute-start.19
  399.1 3.9 collective-permute-start.20
  409.2 15.5 %all-to-all-start.14 = ((f32[4,384,128]{2,1,0:T(8,128)}), f32[4,384,128]{2,1,0:T(8,128)S(1)}, u32[]{:S(2)}, u32[]{:S(2)}) async-start(f32[4,384,128]{2,1,0:T(8,128)} %bitcast.34), calls=%async_computation.14 | async-start | bytes 1572864 | tf_op jit(solution)/shard_map/all_to_all | solution.py:60
  428.7 24.0 %all-to-all-start.15 = ((f32[128,16,128]{2,1,0:T(8,128)}), f32[128,16,128]{2,1,0:T(8,128)S(1)}, u32[]{:S(2)}, u32[]{:S(2)}) async-start(f32[128,16,128]{2,1,0:T(8,128)} %bitcast.35), calls=%async_computation.15 | async-start | bytes 2097152 | tf_op jit(solution)/shard_map/all_to_all | solution.py:284
where the time goes:
time: 457 us; the launch traced here: 455 us
  waiting for transfers between devices  176 us (39%)
  blocking collectives  115 us (25%)
  Pallas kernels  87 us (19%)
  starting transfers between devices  71.8 us (16%)
    all_to_all x7, blocking collectives, exchange(): lax.all_to_all(tiles, AXES, 0, 0, axis_index_groups=same_core_groups(min(...  115 us
    ppermute x21, waiting for transfers between devices, swap(): return lax.ppermute(block, AXES, [(i, i ^ mask) for i in range(count)])  76.9 us
    pallas_call x14, Pallas kernels, stepped(): pl.pallas_call(body, grid_spec=pltpu.PrefetchScalarGridSpec(num_scalar_pr...  63.7 us
    all_to_all x7, waiting for transfers between devices, exchange(): lax.all_to_all(tiles, AXES, 0, 0, axis_index_groups=same_core_groups(min(...  62.4 us
    all_to_all x2, waiting for transfers between devices, move_rows(): return lax.all_to_all(tiles, AXES, 0, 0, tiled=True).reshape(outgoing.shape)  36.8 us
    all_to_all x7, starting transfers between devices, exchange(): lax.all_to_all(tiles, AXES, 0, 0, axis_index_groups=same_core_groups(min(...  29.5 us
    ppermute x21, starting transfers between devices, swap(): return lax.ppermute(block, AXES, [(i, i ^ mask) for i in range(count)])  27.4 us
    all_to_all x2, starting transfers between devices, move_rows(): return lax.all_to_all(tiles, AXES, 0, 0, tiled=True).reshape(outgoing.shape)  14.9 us
  transfers between devices with their start and end apart: 30, of which 22 were waited for; matrix products, arithmetic and copies ran while one was open for 1% of the time, Pallas kernels for 6%

commit v1 on v0

v1 whole, which is shorter than its diff:
```python
import jax
import jax.numpy as jnp
from jax import lax
from jax.experimental import pallas as pl
from jax.experimental.pallas import tpu as pltpu
from jax.sharding import PartitionSpec as P


LEAF_PIV = 384
SEP_PIV = 128
PIVOTS = (LEAF_PIV, SEP_PIV, SEP_PIV, SEP_PIV)
AXES = ("leaf", "front")
F32 = jnp.float32
BF16 = jnp.bfloat16
SLOTS = 16
CHIPS = 4
CORE = 1
PLANE = 32
VMEM = pltpu.VMEM
HBM = pltpu.HBM


def params(mib):
    return pltpu.CompilerParams(vmem_limit_bytes=mib * 2**20)


def on_chip(x):
    return pltpu.with_memory_space_constraint(x, VMEM)


def off_chip(x):
    return pltpu.with_memory_space_constraint(x, HBM)


def vmem_specs(count):
    return [pl.BlockSpec(memory_space=VMEM)] * count


def call(body, outs, *args):
    return pl.pallas_call(
        body,
        in_specs=vmem_specs(len(args)),
        out_specs=vmem_specs(len(outs)),
        out_shape=[VMEM(shape, F32) for shape in outs],
        compiler_params=params(16),
    )(*[on_chip(a) for a in args])


def same_core_groups(height):
    leaves, fronts = lax.axis_size("leaf"), lax.axis_size("front")
    span = 2**height
    return [
        [(base + leaf) * fronts + 2 * chip + core for chip in range(fronts // 2) for leaf in range(span)]
        for base in range(0, leaves, span)
        for core in range(2)
    ]


def exchange(tiles, height):
    return lax.all_to_all(
        tiles, AXES, 0, 0, axis_index_groups=same_core_groups(min(height, 2)), tiled=True
    )


def swap(block, mask):
    count = lax.axis_size("leaf") * lax.axis_size("front")
    return lax.ppermute(block, AXES, [(i, i ^ mask) for i in range(count)])


def pair_of(x):
    high = x.astype(BF16)
    return high, (x - high.astype(F32)).astype(BF16)


def dot(a, b):
    return jnp.dot(a, b, preferred_element_type=F32)


def moves(pieces, at_ref, sources, sends, stages, in_sem, out_sem):
    inward, outward = [], []
    for number, (source, cuts, place) in enumerate(pieces):
        width = stages[number].shape[1] // CHIPS
        inward.append([])
        for chip in range(CHIPS):
            block = 2 * cuts * chip + at_ref[place]
            here = pl.ds(pl.multiple_of(block * width, 128), width)
            inward[-1].append(
                pltpu.make_async_copy(
                    sources[source].at[:, here],
                    stages[number].at[:, pl.ds(chip * width, width)],
                    in_sem.at[number * CHIPS + chip],
                )
            )
        outward.append(pltpu.make_async_copy(stages[number], sends[number], out_sem.at[number]))
    return inward, outward


def cut_sends(places, matrices, pieces, index=None, rows=None):
    shapes = [(matrices[m].shape[0], matrices[m].shape[1] // (2 * cuts)) for m, cuts, _ in pieces]
    count, total = len(pieces), len(matrices)
    extra = [] if rows is None else [index[None, :], rows]

    def body(at_ref, *refs):
        sources, refs = refs[:total], refs[total:]
        given, refs = refs[: len(extra)], refs[len(extra) :]
        sends, refs = refs[:count], refs[count:]
        filled, refs = refs[: len(extra) // 2], refs[len(extra) // 2 :]
        stages, sems = refs[:count], refs[count:]
        inward, outward = moves(pieces, at_ref, sources, sends, stages, *sems)
        for group in inward:
            for copy in group:
                copy.start()
        if extra:
            slots_body(*given, *filled)
        for group, after in zip(inward, outward):
            for copy in group:
                copy.wait()
            after.start()
        for copy in outward:
            copy.wait()

    peers = lax.axis_size("leaf") * lax.axis_size("front")
    slots = [] if rows is None else [VMEM((peers * SLOTS, rows.shape[1]), F32)]
    return pl.pallas_call(
        body,
        in_specs=[pl.BlockSpec(memory_space=pltpu.SMEM)]
        + [pl.BlockSpec(memory_space=HBM)] * total
        + vmem_specs(len(extra)),
        out_specs=[pl.BlockSpec(memory_space=HBM)] * count + vmem_specs(len(slots)),
        out_shape=[HBM(shape, F32) for shape in shapes] + slots,
        scratch_shapes=[VMEM(shape, F32) for shape in shapes]
        + [pltpu.SemaphoreType.DMA((CHIPS * count,)), pltpu.SemaphoreType.DMA((count,))],
        compiler_params=params(20),
    )(places, *[off_chip(m) for m in matrices], *extra)


def shape_of(mats):
    return (len(mats) * mats[1].shape[0], mats[1].shape[1])


def loads(at_ref, sources, held, sem):
    parts = len(sources)
    rows, width = held.shape[0] // parts, held.shape[1] // CHIPS
    cuts = sources[0].shape[1] // (2 * CHIPS * width)

    def copy(part, step):
        there = pl.ds(pl.multiple_of(step * width, 128), width)
        block = 2 * cuts * step + at_ref[cuts - 1] if part == 0 else step
        here = pl.ds(pl.multiple_of(block * width, 128), width)
        return pltpu.make_async_copy(
            sources[part].at[:, here], held.at[pl.ds(part * rows, rows), there], sem.at[part, step]
        )

    def start():
        for step in range(CHIPS):
            for part in range(parts):
                copy(part, step).start()

    def wait(step):
        for part in range(parts):
            copy(part, step).wait()

    return start, wait


def applied(places, mats, vectors, following=None):
    parts, rows, count = len(mats), mats[1].shape[0], vectors.shape[1]
    extra = list(following or [])

    def body(at_ref, *refs):
        sources, later = refs[:parts], refs[parts : parts + len(extra)]
        vec_ref, out_ref, kept_ref = refs[parts + len(extra) : parts + len(extra) + 3]
        acc_ref, sem, late_sem, *spare = refs[parts + len(extra) + 3 :]
        held = spare[0] if extra else kept_ref
        start, wait = loads(at_ref, sources, held, sem)
        start()
        if extra:
            late_start, late_wait = loads(at_ref, later, kept_ref, late_sem)
            late_start()
        width = held.shape[1] // CHIPS
        acc_ref[...] = jnp.zeros(acc_ref.shape, F32)

        @pl.loop(0, CHIPS)
        def _(step):
            wait(step)
            at = pl.ds(pl.multiple_of(step * width, 128), width)
            high, low = pair_of(held[:, at])
            right = jnp.concatenate(pair_of(vec_ref[at, :]), axis=1)
            full = dot(high, right) + dot(low, right)
            acc_ref[...] += full[:, :count] + full[:, count:]

        for part in range(parts):
            out_ref[part] = acc_ref[part * rows : (part + 1) * rows]
        if extra:
            for step in range(CHIPS):
                late_wait(step)

    kept = shape_of(extra or mats)
    return pl.pallas_call(
        body,
        in_specs=[pl.BlockSpec(memory_space=pltpu.SMEM)]
        + [pl.BlockSpec(memory_space=HBM)] * (parts + len(extra))
        + vmem_specs(1),
        out_specs=vmem_specs(2),
        out_shape=[VMEM((parts, rows, count), F32), VMEM(kept, F32)],
        scratch_shapes=[
            VMEM((parts * rows, count), F32),
            pltpu.SemaphoreType.DMA((parts, CHIPS)),
            pltpu.SemaphoreType.DMA((max(1, len(extra)), CHIPS)),
        ]
        + ([VMEM(shape_of(mats), F32)] if extra else []),
        compiler_params=params(20),
    )(places, *[off_chip(m) for m in list(mats) + extra], on_chip(vectors))


def spread(held_ref, vector, out_ref):
    left = jnp.concatenate(pair_of(vector.T), axis=0)
    count, width = vector.shape[1], held_ref.shape[1] // CHIPS

    @pl.loop(0, CHIPS)
    def _(step):
        at = pl.ds(pl.multiple_of(step * width, 128), width)
        up, down = pair_of(held_ref[:, at])
        full = dot(left, up) + dot(left, down)
        out_ref[at, :] = (full[:count] + full[count:]).T


def rows_of(*tiles):
    return jnp.concatenate(tiles, axis=0)


def joined(here_ref, there_ref):
    return rows_of(here_ref[0] + there_ref[1], here_ref[1] + there_ref[0])


def forward_body(held_ref, here_ref, there_ref, out_ref, solved_ref):
    solved = joined(here_ref, there_ref)
    solved_ref[...] = solved
    spread(held_ref, solved, out_ref)


def plane_body(held_ref, solved_ref, far_ref, out_ref):
    spread(held_ref, rows_of(solved_ref[...], far_ref[...]), out_ref)


def top_body(held_ref, here_ref, there_ref, out_ref):
    vector = rows_of(*[here_ref[part] + there_ref[part ^ 2] for part in range(4)])
    spread(held_ref, vector, out_ref)


def backward_body(held_ref, here_ref, there_ref, solved_ref, out_ref):
    spread(held_ref, solved_ref[...] - joined(here_ref, there_ref), out_ref)


def joined_body(here_ref, there_ref, out_ref):
    out_ref[...] = joined(here_ref, there_ref)


def core_pair_body(here_ref, there_ref, out_ref):
    for part in range(4):
        out_ref[part] = here_ref[part] + there_ref[part ^ 1]


def plane_pair_body(here_ref, there_ref, out_ref):
    for part in range(2):
        out_ref[part] = here_ref[part] + there_ref[part]


def minus_sum_body(tiles_ref, base_ref, out_ref):
    share = base_ref[...] - jnp.sum(tiles_ref[...], axis=0)
    out_ref[...] = jnp.broadcast_to(share[None], out_ref.shape)


def sum_body(tiles_ref, share_ref, out_ref):
    share = jnp.sum(tiles_ref[...], axis=0)
    share_ref[...] = share
    out_ref[...] = jnp.broadcast_to(share[None], out_ref.shape)


def slots_body(index_ref, rows_ref, out_ref):
    parts = jnp.concatenate(pair_of(rows_ref[...]), axis=1)
    count, width = rows_ref.shape
    index = index_ref[...]

    @pl.loop(0, out_ref.shape[0] // 512)
    def _(step):
        start = pl.multiple_of(step * 512, 512)
        slot = lax.broadcasted_iota(jnp.int32, (512, count), 0) + start
        chosen = dot((slot == index).astype(F32).astype(BF16), parts)
        out_ref[pl.ds(start, 512), :] = chosen[:, :width] + chosen[:, width:]


def to_slots(index, rows):
    peers = lax.axis_size("leaf") * lax.axis_size("front")
    return pl.pallas_call(
        slots_body,
        in_specs=vmem_specs(2),
        out_specs=pl.BlockSpec(memory_space=VMEM),
        out_shape=VMEM((peers * SLOTS, rows.shape[1]), F32),
        compiler_params=params(16),
    )(index[None, :], rows)


def rank_among(keys, order):
    same = (keys[:, None] == keys[None, :]) & (order[None, :] < order[:, None])
    return jnp.sum(same.astype(jnp.int32), axis=1)


def move_rows(outgoing):
    tiles = outgoing.reshape(-1, SLOTS, outgoing.shape[1])
    return lax.all_to_all(tiles, AXES, 0, 0, tiled=True).reshape(outgoing.shape)


def whole_solve(app_rhs, pivot_source, row_owner, *matrices):
    core = lax.axis_index("front") % 2
    plane = lax.axis_index("leaf") // 4 % 2
    row_count, width = app_rhs.shape
    matrices = [m[0, 0] for m in matrices]

    destination = row_owner // row_count
    send_index = destination * SLOTS + rank_among(
        destination, jnp.arange(row_count, dtype=jnp.int32)
    )
    anchor = pivot_source // row_count
    recv_index = anchor * SLOTS + rank_among(anchor, pivot_source)

    def all_places(core, plane):
        near, far = 2 * core + plane, 2 * (1 - core) + plane
        table = [core, near, 1 - core, far, near + 1 - 2 * plane, far + 1 - 2 * plane]
        return jnp.stack(table).astype(jnp.int32)

    places = all_places(core, plane)
    first = [(0, 1, 2), (1, 1, 2)]
    *sends, outgoing = cut_sends(places, matrices[:2], first, send_index, app_rhs)
    mats = [[matrices[m], swap(sends[m], CORE)] for m in range(2)]
    ordered = move_rows(outgoing)[recv_index]
    ordered, core, plane = lax.optimization_barrier((ordered, core, plane))
    late = [(m, 1, 2) for m in range(3)] + [(m, 2, p) for m in (3, 4) for p in (3, 4, 5)]
    sends = cut_sends(all_places(core, plane), matrices[2:], late)
    mats += [[matrices[m], swap(sends[m - 2], CORE)] for m in range(2, 5)]
    mats += [[matrices[m], swap(sends[3 * m - 12], CORE)] for m in (5, 6)]
    for number, piece in enumerate((4, 5, 7, 8)):
        half = swap(sends[piece], (PLANE, PLANE | CORE)[number % 2])
        mats[5 + number // 2].append(half)
    inverses = (mats[0], mats[2], mats[4], mats[6])
    couplings = (mats[1], mats[3], mats[5])

    starts = (0, LEAF_PIV, LEAF_PIV + SEP_PIV, LEAF_PIV + 2 * SEP_PIV)
    sizes = (CHIPS, 2 * CHIPS, 4 * CHIPS, 4 * CHIPS)
    own = [ordered[at : at + rows] for at, rows in zip(starts, PIVOTS)]
    tiles = jnp.broadcast_to(own[0][None], (sizes[0], LEAF_PIV, width))
    solved = []
    for height in range(3):
        gathered = exchange(tiles, height).reshape(-1, width)
        here, held = applied(places, inverses[height], gathered, couplings[height])
        there = swap(here, CORE)
        outs = [(held.shape[1], width), (2 * PIVOTS[height], width)]
        if height < 2:
            carried, forward = call(forward_body, outs, held, here, there)
        else:
            (forward,) = call(joined_body, outs[1:], here, there)
            (carried,) = call(plane_body, outs[:1], held, forward, swap(forward, PLANE))
        solved.append(forward)
        arrived = exchange(carried.reshape(-1, SEP_PIV, width), height + 1)
        (tiles,) = call(
            minus_sum_body, [(sizes[height + 1], SEP_PIV, width)], arrived, own[height + 1]
        )
    here, held = applied(places, inverses[3], exchange(tiles, 3).reshape(-1, width))
    (here,) = call(core_pair_body, [here.shape], here, swap(here, CORE))
    (spread_out,) = call(top_body, [(held.shape[1], width)], held, here, swap(here, PLANE))
    pieces = [None, None, None, None]
    for height in (3, 2, 1):
        arrived = exchange(spread_out.reshape(-1, SEP_PIV, width), height)
        pieces[height], tiles = call(
            sum_body, [(SEP_PIV, width), (sizes[height], SEP_PIV, width)], arrived
        )
        parent = exchange(tiles, height).reshape(-1, width)
        here, held = applied(places, couplings[height - 1], parent, inverses[height - 1])
        if height == 3:
            (here,) = call(plane_pair_body, [(2, SEP_PIV, width)], here, swap(here[2:], PLANE))
        there = swap(here, CORE)
        (spread_out,) = call(
            backward_body, [(held.shape[1], width)], held, here, there, solved[height - 1]
        )
    pieces[0] = exchange(spread_out.reshape(-1, LEAF_PIV, width), 0).sum(axis=0)
    pivot_order = jnp.concatenate(pieces, axis=0)
    return move_rows(to_slots(recv_index, pivot_order))[send_index]


def solution(mesh):
    wide = P("leaf", "front", None, None)
    in_specs = (P(AXES, None), P(AXES), P(AXES)) + (wide,) * 7
    return jax.shard_map(
        whole_solve, mesh=mesh, in_specs=in_specs, out_specs=P(AXES, None), check_vma=False
    )
```

time: 457 us -> 429 us (0.939)
  Pallas kernels: 87 us -> 63.6 us
  blocking collectives: 115 us -> 101 us
  waiting for transfers between devices: 176 us -> 182 us
    pallas_call x16 -> x9, Pallas kernels: 75.6 us -> 39.2 us  [the longest x7 26.1 us: applied(): pl.pallas_call(body, in_specs=[pl.BlockSpec(memory_space=pltpu.SMEM)] + [...]
    pallas_call x9 -> x16, Pallas kernels: 3.41 us -> 21.7 us  [call(): pl.pallas_call(body, in_specs=vmem_specs(len(args)), out_specs=vmem_specs...]
    all_to_all x7 -> x6, blocking collectives: 115 us -> 101 us  [exchange(): lax.all_to_all(tiles, AXES, 0, 0, axis_index_groups=same_core_groups(min(...]
    pallas_call x2 -> x1, Pallas kernels: 7.98 us -> 2.6 us  [to_slots(): pl.pallas_call(slots_body, in_specs=vmem_specs(2), out_specs=pl.BlockSpec...]
    all_to_all x7 -> x8, waiting for transfers between devices: 62.4 us -> 66.8 us  [exchange(): lax.all_to_all(tiles, AXES, 0, 0, axis_index_groups=same_core_groups(min(...]
    all_to_all x7 -> x8, starting transfers between devices: 29.5 us -> 32.3 us  [exchange(): lax.all_to_all(tiles, AXES, 0, 0, axis_index_groups=same_core_groups(min(...]
  transfers between devices with their start and end apart: 30 -> 31, of which waited for: 22 -> 21; matrix products, arithmetic and copies ran while one was open for 1% -> 1% of each run, Pallas kernels for 6% -> 3%
where the time goes in v1:
time: 429 us; the launch traced here: 428 us
  waiting for transfers between devices  182 us (42%)
  blocking collectives  101 us (24%)
  starting transfers between devices  70.6 us (16%)
  Pallas kernels  63.6 us (15%)
  local copies, waits for them, and re-layouts  7.72 us (2%)
    all_to_all x6, blocking collectives, exchange(): lax.all_to_all(tiles, AXES, 0, 0, axis_index_groups=same_core_groups(min(...  101 us
    ppermute x21, waiting for transfers between devices, swap(): return lax.ppermute(block, AXES, [(i, i ^ mask) for i in range(count)])  78.5 us
    all_to_all x8, waiting for transfers between devices, exchange(): lax.all_to_all(tiles, AXES, 0, 0, axis_index_groups=same_core_groups(min(...  66.8 us
    all_to_all x2, waiting for transfers between devices, move_rows(): return lax.all_to_all(tiles, AXES, 0, 0, tiled=True).reshape(outgoing.shape)  36.8 us
    all_to_all x8, starting transfers between devices, exchange(): lax.all_to_all(tiles, AXES, 0, 0, axis_index_groups=same_core_groups(min(...  32.3 us
    pallas_call x7, Pallas kernels, applied(): pl.pallas_call(body, in_specs=[pl.BlockSpec(memory_space=pltpu.SMEM)] + [...  26.1 us
    ppermute x21, starting transfers between devices, swap(): return lax.ppermute(block, AXES, [(i, i ^ mask) for i in range(count)])  23.4 us
    pallas_call x16, Pallas kernels, call(): pl.pallas_call(body, in_specs=vmem_specs(len(args)), out_specs=vmem_specs...  21.7 us
  transfers between devices with their start and end apart: 31, of which 21 were waited for; matrix products, arithmetic and copies ran while one was open for 1% of the time, Pallas kernels for 3%

profile of v1, /device:TPU:1, one launch (start us, length us, event | category | flops | bytes accessed | tf_op | source)
XLA Modules:
  0.0 427.5 jit_solution(16647212521812505771)
XLA Ops:
  2.9 5.1 %shard_map.100 = (f32[384,1536]{1,0:T(8,128)}, f32[384,1024]{1,0:T(8,128)}, f32[2048,128]{1,0:T(8,128)}) custom-call(s32[6]{0:T(128)S(1)} %stack.48.at_ref, f32[384,3072]{1,0:T(8,128)} %bitcast.47, f32[384,2048]{1,0:T(8,128)} %bitcast.53, s32[1,768]{1,0:T(1,128)S(1)} %broadcast_in_dim.11.refs_2_, f32[768,128]{1,0:T(8,128)S(1)} %copy-done.2), custom_call_target="tpu_custom_call" | custom-call | tf_op jit(solution)/shard_map/pallas_call | solution.py:124
  8.0 1.5 collective-permute-start.1
  9.5 10.2 %all-to-all-start = ((f32[128,16,128]{2,1,0:T(8,128)}), f32[128,16,128]{2,1,0:T(8,128)S(1)}, u32[]{:S(2)}, u32[]{:S(2)}) async-start(f32[128,16,128]{2,1,0:T(8,128)} %bitcast.9), calls=%async_computation | async-start | bytes 2097152 | tf_op jit(solution)/shard_map/all_to_all | solution.py:311
  19.7 1.1 collective-permute-start
  21.4 17.5 %all-to-all-done = f32[128,16,128]{2,1,0:T(8,128)S(1)} async-done(((f32[128,16,128]{2,1,0:T(8,128)}), f32[128,16,128]{2,1,0:T(8,128)S(1)}, u32[]{:S(2)}, u32[]{:S(2)}) %all-to-all-start) | async-done | bytes 1048608 | tf_op jit(solution)/shard_map/all_to_all | solution.py:311
  38.9 1.6 gather_fusion
  41.5 3.5 all-to-all-start.1
  45.1 11.4 %all-to-all-done.1 = f32[4,384,128]{2,1,0:T(8,128)S(1)} async-done(((f32[4,384,128]{2,1,0:T(8,128)}), f32[4,384,128]{2,1,0:T(8,128)S(1)}, u32[]{:S(2)}, u32[]{:S(2)}) %all-to-all-start.1) | async-done | bytes 786464 | tf_op jit(solution)/shard_map/all_to_all | solution.py:60
  56.4 4.5 %shard_map.102 = (f32[2,384,128]{2,1,0:T(8,128)S(1)}, f32[768,1024]{1,0:T(8,128)S(1)}) custom-call(s32[6]{0:T(128)S(1)} %stack.48.at_ref, f32[384,3072]{1,0:T(8,128)} %bitcast.48, f32[384,1536]{1,0:T(8,128)} %collective-permute-done.1.refs_1_.refs_3_, f32[384,2048]{1,0:T(8,128)} %bitcast.54, f32[384,1024]{1,0:T(8,128)} %copy-done.3, f32[1536,128]{1,0:T(8,128)S(1)} %bitcast.43), custom_call_target="tpu_custom_call" | custom-call | tf_op jit(solution)/shard_map/pallas_call | solution.py:199
  60.9 1.6 copy-done
  62.5 1.8 collective-permute-start.11
  64.4 8.0 %shard_map.101 = (f32[128,1024]{1,0:T(8,128)}, f32[128,2048]{1,0:T(8,128)}, f32[128,2048]{1,0:T(8,128)}, f32[128,2048]{1,0:T(8,128)}, f32[128,2048]{1,0:T(8,128)...) custom-call(s32[6]{0:T(128)S(1)} %stack.55.at_ref, ...), custom_call_target="tpu_custom_call" | custom-call | tf_op jit(solution)/shard_map/pallas_call | solution.py:124
  72.6 2.8 shard_map.103
  75.4 3.5 all-to-all-start.2
  79.5 8.5 %all-to-all-done.2.tiles_ref = f32[8,128,128]{2,1,0:T(8,128)S(1)} async-done(((f32[8,128,128]{2,1,0:T(8,128)}), f32[8,128,128]{2,1,0:T(8,128)S(1)}, u32[]{:S(2)}, u32[]{:S(2)}) %all-to-all-start.2) | async-done | bytes 524320 | tf_op jit(solution)/shard_map/all_to_all | solution.py:60
  88.8 3.5 all-to-all-start.3
  92.4 8.5 %all-to-all-done.3 = f32[8,128,128]{2,1,0:T(8,128)S(1)} async-done(((f32[8,128,128]{2,1,0:T(8,128)}), f32[8,128,128]{2,1,0:T(8,128)S(1)}, u32[]{:S(2)}, u32[]{:S(2)}) %all-to-all-start.3) | async-done | bytes 524320 | tf_op jit(solution)/shard_map/all_to_all | solution.py:60
  100.8 2.8 shard_map.105
  103.6 1.9 collective-permute-start.12
  106.5 2.8 shard_map.106
  109.3 3.7 all-to-all-start.4
  113.4 1.8 collective-permute-start.6
  115.3 14.1 %all-to-all-done.4.tiles_ref = f32[16,128,128]{2,1,0:T(8,128)S(1)} async-done(((f32[16,128,128]{2,1,0:T(8,128)}), f32[16,128,128]{2,1,0:T(8,128)S(1)}, u32[]{:S(2)}, u32[]{:S(2)}) %all-to-all-start.4) | async-done | bytes 1048608 | tf_op jit(solution)/shard_map/all_to_all | solution.py:60
  130.5 4.0 all-to-all-start.5
  134.6 3.7 collective-permute-done.5.refs_4_.refs_2_
  138.3 22.8 %collective-permute-done.6.refs_5_.refs_3_ = f32[128,2048]{1,0:T(8,128)} collective-permute-done((f32[128,2048]{1,0:T(8,128)}, f32[128,2048]{1,0:T(8,128)}, u32[]{:S(2)}, u32[]{:S(2)}) %collective-permute-start.6) | collective-permute-done | bytes 1048608 | tf_op jit(solution)/shard_map/ppermute | solution.py:67
  161.1 3.8 shard_map.108
  165.1 1.3 collective-permute-done.13.there_ref
  166.5 4.9 %collective-permute-done.14.far_ref = f32[256,128]{1,0:T(8,128)S(1)} collective-permute-done((f32[256,128]{1,0:T(8,128)S(1)}, f32[256,128]{1,0:T(8,128)S(1)}, u32[]{:S(2)}, u32[]{:S(2)}) %collective-permute-start.14) | collective-permute-done | bytes 131104 | tf_op jit(solution)/shard_map/ppermute | solution.py:67
  171.4 3.4 shard_map.110
  174.7 6.8 %all-to-all-start.6 = ((f32[16,128,128]{2,1,0:T(8,128)}), f32[16,128,128]{2,1,0:T(8,128)S(1)}, u32[]{:S(2)}, u32[]{:S(2)}) async-start(f32[16,128,128]{2,1,0:T(8,128)} %bitcast.26), calls=%async_computation.6 | async-start | bytes 2097152 | tf_op jit(solution)/shard_map/all_to_all | solution.py:60
  181.5 1.4 collective-permute-start.8
  182.9 1.7 collective-permute-start.10
  184.6 12.4 %all-to-all-done.6.tiles_ref = f32[16,128,128]{2,1,0:T(8,128)S(1)} async-done(((f32[16,128,128]{2,1,0:T(8,128)}), f32[16,128,128]{2,1,0:T(8,128)S(1)}, u32[]{:S(2)}, u32[]{:S(2)}) %all-to-all-start.6) | async-done | bytes 1048608 | tf_op jit(solution)/shard_map/all_to_all | solution.py:60
  198.1 3.8 all-to-all-start.7
  202.0 5.9 %collective-permute-done.9.refs_2_ = f32[128,2048]{1,0:T(8,128)} collective-permute-done((f32[128,2048]{1,0:T(8,128)}, f32[128,2048]{1,0:T(8,128)}, u32[]{:S(2)}, u32[]{:S(2)}) %collective-permute-start.9) | collective-permute-done | bytes 1048608 | tf_op jit(solution)/shard_map/ppermute | solution.py:67
  207.8 22.7 %collective-permute-done.10.refs_3_ = f32[128,2048]{1,0:T(8,128)} collective-permute-done((f32[128,2048]{1,0:T(8,128)}, f32[128,2048]{1,0:T(8,128)}, u32[]{:S(2)}, u32[]{:S(2)}) %collective-permute-start.10) | collective-permute-done | bytes 1048608 | tf_op jit(solution)/shard_map/ppermute | solution.py:67
  230.6 3.8 shard_map.112
  234.7 1.4 collective-permute-done.15.there_ref
  236.3 7.7 %collective-permute-done.16.there_ref = f32[4,128,128]{2,1,0:T(8,128)S(1)} collective-permute-done((f32[4,128,128]{2,1,0:T(8,128)S(1)}, f32[4,128,128]{2,1,0:T(8,128)S(1)}, u32[]{:S(2)}, u32[]{:S(2)}) %collective-permute-start.16) | collective-permute-done | bytes 262176 | tf_op jit(solution)/shard_map/ppermute | solution.py:67
  244.0 2.4 shard_map.114
  246.4 22.2 %all_to_all.80.tiles_ref = f32[16,128,128]{2,1,0:T(8,128)S(1)} all-to-all(f32[16,128,128]{2,1,0:T(8,128)S(1)} %bitcast.42), channel_id=1, replica_groups={{0,8,16,24,2,10,18,26,4,12,20,28,6,14,22,30},{1,9,17,25,3,11,19,27,5,13..., dimensions={0} | all-to-all | bytes 2097152 | tf_op jit(solution)/shard_map/all_to_all | solution.py:60
  268.8 18.4 %all_to_all.81 = f32[16,128,128]{2,1,0:T(8,128)S(1)} all-to-all(f32[16,128,128]{2,1,0:T(8,128)S(1)} %get-tuple-element.69), channel_id=1, replica_groups={{0,8,16,24,2,10,18,26,4,12,20,28,6,14,22,30},{1,9,17,25,3,11,19,27,5,13..., dimensions={0} | all-to-all | bytes 2097152 | tf_op jit(solution)/shard_map/all_to_all | solution.py:60
  287.1 3.9 shard_map.116
  291.2 3.8 collective-permute-done.17.there_ref
  295.0 4.3 %collective-permute-start.18 = (f32[2,128,128]{2,1,0:T(8,128)S(1)}, f32[2,128,128]{2,1,0:T(8,128)S(1)}, u32[]{:S(2)}, u32[]{:S(2)}) collective-permute-start(f32[2,128,128]{2,1,0:T(8,128)S(1)} %shard_map.117.here_ref), channel_id=1, source_target_pairs={{0,1},{1,0},{2,3},{3,2},{4,5},{5,4},{6,7},{7,6},{8,9},{9,8},{10,11... | collective-permute-start | bytes 393224 | tf_op jit(solution)/shard_map/ppermute | solution.py:67
  300.3 1.8 shard_map.118
  302.1 19.1 %all_to_all.82.tiles_ref = f32[16,128,128]{2,1,0:T(8,128)S(1)} all-to-all(f32[16,128,128]{2,1,0:T(8,128)S(1)} %bitcast.40), channel_id=1, replica_groups={{0,8,16,24,2,10,18,26,4,12,20,28,6,14,22,30},{1,9,17,25,3,11,19,27,5,13..., dimensions={0} | all-to-all | bytes 2097152 | tf_op jit(solution)/shard_map/all_to_all | solution.py:60
  321.3 18.3 %all_to_all.83 = f32[16,128,128]{2,1,0:T(8,128)S(1)} all-to-all(f32[16,128,128]{2,1,0:T(8,128)S(1)} %get-tuple-element.72), channel_id=1, replica_groups={{0,8,16,24,2,10,18,26,4,12,20,28,6,14,22,30},{1,9,17,25,3,11,19,27,5,13..., dimensions={0} | all-to-all | bytes 2097152 | tf_op jit(solution)/shard_map/all_to_all | solution.py:60
  339.7 3.1 shard_map.120
  342.8 3.3 collective-permute-start.19
  347.1 1.3 shard_map.121
  348.4 11.7 %all_to_all.84.tiles_ref = f32[8,128,128]{2,1,0:T(8,128)S(1)} all-to-all(f32[8,128,128]{2,1,0:T(8,128)S(1)} %bitcast.45), channel_id=1, replica_groups={{0,8,2,10,4,12,6,14},{1,9,3,11,5,13,7,15},{16,24,18,26,20,28,22,30},{17..., dimensions={0} | all-to-all | bytes 1048576 | tf_op jit(solution)/shard_map/all_to_all | solution.py:60
  360.2 11.0 %all_to_all.85 = f32[8,128,128]{2,1,0:T(8,128)S(1)} all-to-all(f32[8,128,128]{2,1,0:T(8,128)S(1)} %get-tuple-element.76), channel_id=1, replica_groups={{0,8,2,10,4,12,6,14},{1,9,3,11,5,13,7,15},{16,24,18,26,20,28,22,30},{17..., dimensions={0} | all-to-all | bytes 1048576 | tf_op jit(solution)/shard_map/all_to_all | solution.py:60
  371.2 4.2 shard_map.123
  375.4 2.5 collective-permute-start.20
  377.9 1.3 collective-permute-done.20.there_ref
  379.2 3.9 shard_map.124
  383.1 3.5 all-to-all-start.14
  386.6 12.0 %all-to-all-done.14 = f32[4,384,128]{2,1,0:T(8,128)S(1)} async-done(((f32[4,384,128]{2,1,0:T(8,128)}), f32[4,384,128]{2,1,0:T(8,128)S(1)}, u32[]{:S(2)}, u32[]{:S(2)}) %all-to-all-start.14) | async-done | bytes 786464 | tf_op jit(solution)/shard_map/all_to_all | solution.py:60
  398.6 2.6 shard_map.125
  401.2 4.7 %all-to-all-start.15 = ((f32[128,16,128]{2,1,0:T(8,128)}), f32[128,16,128]{2,1,0:T(8,128)S(1)}, u32[]{:S(2)}, u32[]{:S(2)}) async-start(f32[128,16,128]{2,1,0:T(8,128)} %bitcast.35), calls=%async_computation.15 | async-start | bytes 2097152 | tf_op jit(solution)/shard_map/all_to_all | solution.py:311
  405.9 19.3 %all-to-all-done.15 = f32[128,16,128]{2,1,0:T(8,128)S(1)} async-done(((f32[128,16,128]{2,1,0:T(8,128)}), f32[128,16,128]{2,1,0:T(8,128)S(1)}, u32[]{:S(2)}, u32[]{:S(2)}) %all-to-all-start.15) | async-done | bytes 1048608 | tf_op jit(solution)/shard_map/all_to_all | solution.py:311
  425.3 2.3 gather_fusion.1
  (72 shorter events, 13.1 us)
Async XLA Ops:
  1.9 1.0 copy-start.2
  2.9 18.0 %copy-start.10 = (s32[768]{0:T(1024)S(1)}, s32[768]{0:T(1024)}, u32[]{:S(2)}) copy-start(s32[768]{0:T(1024)} %param.11) | copy-start | bytes 9220
  8.0 48.4 %collective-permute-start.1 = (f32[384,1536]{1,0:T(8,128)}, f32[384,1536]{1,0:T(8,128)}, u32[]{:S(2)}, u32[]{:S(2)}) collective-permute-start(f32[384,1536]{1,0:T(8,128)} %get-tuple-element.45), channel_id=1, source_target_pairs={{0,1},{1,0},{2,3},{3,2},{4,5},{5,4},{6,7},{7,6},{8,9},{9,8},{10,11... | collective-permute-start | bytes 7077896 | tf_op jit(solution)/shard_map/ppermute | solution.py:67
  9.5 29.5 %all-to-all-start = ((f32[128,16,128]{2,1,0:T(8,128)}), f32[128,16,128]{2,1,0:T(8,128)S(1)}, u32[]{:S(2)}, u32[]{:S(2)}) async-start(f32[128,16,128]{2,1,0:T(8,128)} %bitcast.9), calls=%async_computation | async-start | bytes 2097152 | tf_op jit(solution)/shard_map/all_to_all | solution.py:311
  19.7 25.3 %collective-permute-start = (f32[384,1024]{1,0:T(8,128)}, f32[384,1024]{1,0:T(8,128)S(1)}, u32[]{:S(2)}, u32[]{:S(2)}) collective-permute-start(f32[384,1024]{1,0:T(8,128)} %get-tuple-element.44), channel_id=1, source_target_pairs={{0,1},{1,0},{2,3},{3,2},{4,5},{5,4},{6,7},{7,6},{8,9},{9,8},{10,11... | collective-permute-start | bytes 4718600 | tf_op jit(solution)/shard_map/ppermute | solution.py:67
  40.5 20.4 %copy-start.7 = (f32[768,128]{1,0:T(8,128)}, f32[768,128]{1,0:T(8,128)S(1)}, u32[]{:S(2)}) copy-start(f32[768,128]{1,0:T(8,128)S(1)} %gather_fusion) | copy-start | bytes 1179652
  41.5 14.9 %all-to-all-start.1 = ((f32[4,384,128]{2,1,0:T(8,128)}), f32[4,384,128]{2,1,0:T(8,128)S(1)}, u32[]{:S(2)}, u32[]{:S(2)}) async-start(f32[4,384,128]{2,1,0:T(8,128)} %broadcast_in_dim.13), calls=%async_computation.1 | async-start | bytes 1572864 | tf_op jit(solution)/shard_map/all_to_all | solution.py:60
  45.0 11.4 %copy-start.3 = (f32[384,1024]{1,0:T(8,128)}, f32[384,1024]{1,0:T(8,128)S(1)}, u32[]{:S(2)}) copy-start(f32[384,1024]{1,0:T(8,128)S(1)} %collective-permute-done.refs_3_.refs_1_) | copy-start | bytes 4718596
  60.9 1.6 copy-start
  62.5 10.0 %collective-permute-start.11 = (f32[2,384,128]{2,1,0:T(8,128)S(1)}, f32[2,384,128]{2,1,0:T(8,128)S(1)}, u32[]{:S(2)}, u32[]{:S(2)}) collective-permute-start(f32[2,384,128]{2,1,0:T(8,128)S(1)} %get-tuple-element.60.here_ref), channel_id=1, source_target_pairs={{0,1},{1,0},{2,3},{3,2},{4,5},{5,4},{6,7},{7,6},{8,9},{9,8},{10,11... | collective-permute-start | bytes 1179656 | tf_op jit(solution)/shard_map/ppermute | solution.py:67
  64.4 8.1 %copy-start.1 = (f32[768,1024]{1,0:T(8,128)S(1)}, f32[768,1024]{1,0:T(8,128)}, u32[]{:S(2)}) copy-start(f32[768,1024]{1,0:T(8,128)} %copy-done) | copy-start | bytes 9437188
  72.5 19.9 %collective-permute-start.2 = (f32[128,2048]{1,0:T(8,128)}, f32[128,2048]{1,0:T(8,128)S(1)}, u32[]{:S(2)}, u32[]{:S(2)}) collective-permute-start(f32[128,2048]{1,0:T(8,128)} %get-tuple-element.49), channel_id=1, source_target_pairs={{0,1},{1,0},{2,3},{3,2},{4,5},{5,4},{6,7},{7,6},{8,9},{9,8},{10,11... | collective-permute-start | bytes 3145736 | tf_op jit(solution)/shard_map/ppermute | solution.py:67
  72.6 6.9 %copy-start.8 = (f32[768,128]{1,0:T(8,128)S(1)}, f32[768,128]{1,0:T(8,128)}, u32[]{:S(2)}) copy-start(f32[768,128]{1,0:T(8,128)} %copy-done.7) | copy-start | bytes 1179652
  75.4 12.6 %all-to-all-start.2 = ((f32[8,128,128]{2,1,0:T(8,128)}), f32[8,128,128]{2,1,0:T(8,128)S(1)}, u32[]{:S(2)}, u32[]{:S(2)}) async-start(f32[8,128,128]{2,1,0:T(8,128)} %bitcast.22), calls=%async_computation.2 | async-start | bytes 1048576 | tf_op jit(solution)/shard_map/all_to_all | solution.py:60
  78.9 13.4 %collective-permute-start.3 = (f32[128,1024]{1,0:T(8,128)}, f32[128,1024]{1,0:T(8,128)S(1)}, u32[]{:S(2)}, u32[]{:S(2)}) collective-permute-start(f32[128,1024]{1,0:T(8,128)} %get-tuple-element.50), channel_id=1, source_target_pairs={{0,1},{1,0},{2,3},{3,2},{4,5},{5,4},{6,7},{7,6},{8,9},{9,8},{10,11... | collective-permute-start | bytes 1572872 | tf_op jit(solution)/shard_map/ppermute | solution.py:67
  88.8 12.0 %all-to-all-start.3 = ((f32[8,128,128]{2,1,0:T(8,128)}), f32[8,128,128]{2,1,0:T(8,128)S(1)}, u32[]{:S(2)}, u32[]{:S(2)}) async-start(f32[8,128,128]{2,1,0:T(8,128)} %shard_map.104), calls=%async_computation.3 | async-start | bytes 1048576 | tf_op jit(solution)/shard_map/all_to_all | solution.py:60
  92.3 8.5 %copy-start.6 = (f32[128,1024]{1,0:T(8,128)}, f32[128,1024]{1,0:T(8,128)S(1)}, u32[]{:S(2)}) copy-start(f32[128,1024]{1,0:T(8,128)S(1)} %collective-permute-done.3.refs_1_.refs_3_) | copy-start | bytes 1572868
  92.4 8.5 %copy-start.5 = (f32[128,2048]{1,0:T(8,128)}, f32[128,2048]{1,0:T(8,128)S(1)}, u32[]{:S(2)}) copy-start(f32[128,2048]{1,0:T(8,128)S(1)} %collective-permute-done.2.refs_3_.refs_1_) | copy-start | bytes 3145732
  103.6 2.9 collective-permute-start.12
  109.3 20.1 %all-to-all-start.4 = ((f32[16,128,128]{2,1,0:T(8,128)}), f32[16,128,128]{2,1,0:T(8,128)S(1)}, u32[]{:S(2)}, u32[]{:S(2)}) async-start(f32[16,128,128]{2,1,0:T(8,128)} %bitcast.24), calls=%async_computation.4 | async-start | bytes 2097152 | tf_op jit(solution)/shard_map/all_to_all | solution.py:60
  113.0 21.6 %collective-permute-start.4 = (f32[128,2048]{1,0:T(8,128)}, f32[128,2048]{1,0:T(8,128)S(1)}, u32[]{:S(2)}, u32[]{:S(2)}) collective-permute-start(f32[128,2048]{1,0:T(8,128)} %get-tuple-element.51), channel_id=1, source_target_pairs={{0,1},{1,0},{2,3},{3,2},{4,5},{5,4},{6,7},{7,6},{8,9},{9,8},{10,11... | collective-permute-start | bytes 3145736 | tf_op jit(solution)/shard_map/ppermute | solution.py:67
  113.4 24.9 %collective-permute-start.5 = (f32[128,2048]{1,0:T(8,128)}, f32[128,2048]{1,0:T(8,128)}, u32[]{:S(2)}, u32[]{:S(2)}) collective-permute-start(f32[128,2048]{1,0:T(8,128)} %get-tuple-element.52), channel_id=1, source_target_pairs={{0,32},{1,33},{2,34},{3,35},{4,36},{5,37},{6,38},{7,39},{8,40},{9,... | collective-permute-start | bytes 3145736 | tf_op jit(solution)/shard_map/ppermute | solution.py:67
  113.4 47.7 %collective-permute-start.6 = (f32[128,2048]{1,0:T(8,128)}, f32[128,2048]{1,0:T(8,128)}, u32[]{:S(2)}, u32[]{:S(2)}) collective-permute-start(f32[128,2048]{1,0:T(8,128)} %get-tuple-element.53), channel_id=1, source_target_pairs={{0,33},{1,32},{2,35},{3,34},{4,37},{5,36},{6,39},{7,38},{8,41},{9,... | collective-permute-start | bytes 3145736 | tf_op jit(solution)/shard_map/ppermute | solution.py:67
  115.2 45.9 %collective-permute-start.7 = (f32[128,2048]{1,0:T(8,128)}, f32[128,2048]{1,0:T(8,128)}, u32[]{:S(2)}, u32[]{:S(2)}) collective-permute-start(f32[128,2048]{1,0:T(8,128)} %get-tuple-element.54), channel_id=1, source_target_pairs={{0,1},{1,0},{2,3},{3,2},{4,5},{5,4},{6,7},{7,6},{8,9},{9,8},{10,11... | collective-permute-start | bytes 3145736 | tf_op jit(solution)/shard_map/ppermute | solution.py:67
  130.5 30.6 %all-to-all-start.5 = ((f32[16,128,128]{2,1,0:T(8,128)}), f32[16,128,128]{2,1,0:T(8,128)S(1)}, u32[]{:S(2)}, u32[]{:S(2)}) async-start(f32[16,128,128]{2,1,0:T(8,128)} %shard_map.107), calls=%async_computation.5 | async-start | bytes 2097152 | tf_op jit(solution)/shard_map/all_to_all | solution.py:60
  134.6 26.5 %copy-start.4 = (f32[128,2048]{1,0:T(8,128)}, f32[128,2048]{1,0:T(8,128)S(1)}, u32[]{:S(2)}) copy-start(f32[128,2048]{1,0:T(8,128)S(1)} %collective-permute-done.4.refs_3_.refs_1_) | copy-start | bytes 3145732
  164.9 1.4 collective-permute-start.13
  166.4 5.0 %collective-permute-start.14 = (f32[256,128]{1,0:T(8,128)S(1)}, f32[256,128]{1,0:T(8,128)S(1)}, u32[]{:S(2)}, u32[]{:S(2)}) collective-permute-start(f32[256,128]{1,0:T(8,128)S(1)} %shard_map.109.solved_ref), channel_id=1, source_target_pairs={{0,32},{1,33},{2,34},{3,35},{4,36},{5,37},{6,38},{7,39},{8,40},{9,... | collective-permute-start | bytes 393224 | tf_op jit(solution)/shard_map/ppermute | solution.py:67
  174.7 22.3 %all-to-all-start.6 = ((f32[16,128,128]{2,1,0:T(8,128)}), f32[16,128,128]{2,1,0:T(8,128)S(1)}, u32[]{:S(2)}, u32[]{:S(2)}) async-start(f32[16,128,128]{2,1,0:T(8,128)} %bitcast.26), calls=%async_computation.6 | async-start | bytes 2097152 | tf_op jit(solution)/shard_map/all_to_all | solution.py:60
  181.5 20.4 %collective-permute-start.8 = (f32[128,2048]{1,0:T(8,128)}, f32[128,2048]{1,0:T(8,128)S(1)}, u32[]{:S(2)}, u32[]{:S(2)}) collective-permute-start(f32[128,2048]{1,0:T(8,128)} %get-tuple-element.55), channel_id=1, source_target_pairs={{0,1},{1,0},{2,3},{3,2},{4,5},{5,4},{6,7},{7,6},{8,9},{9,8},{10,11... | collective-permute-start | bytes 3145736 | tf_op jit(solution)/shard_map/ppermute | solution.py:67
  182.9 24.9 %collective-permute-start.9 = (f32[128,2048]{1,0:T(8,128)}, f32[128,2048]{1,0:T(8,128)}, u32[]{:S(2)}, u32[]{:S(2)}) collective-permute-start(f32[128,2048]{1,0:T(8,128)} %get-tuple-element.56), channel_id=1, source_target_pairs={{0,32},{1,33},{2,34},{3,35},{4,36},{5,37},{6,38},{7,39},{8,40},{9,... | collective-permute-start | bytes 3145736 | tf_op jit(solution)/shard_map/ppermute | solution.py:67
  182.9 47.7 %collective-permute-start.10 = (f32[128,2048]{1,0:T(8,128)}, f32[128,2048]{1,0:T(8,128)}, u32[]{:S(2)}, u32[]{:S(2)}) collective-permute-start(f32[128,2048]{1,0:T(8,128)} %get-tuple-element.57), channel_id=1, source_target_pairs={{0,33},{1,32},{2,35},{3,34},{4,37},{5,36},{6,39},{7,38},{8,41},{9,... | collective-permute-start | bytes 3145736 | tf_op jit(solution)/shard_map/ppermute | solution.py:67
  198.1 32.5 %all-to-all-start.7 = ((f32[16,128,128]{2,1,0:T(8,128)}), f32[16,128,128]{2,1,0:T(8,128)S(1)}, u32[]{:S(2)}, u32[]{:S(2)}) async-start(f32[16,128,128]{2,1,0:T(8,128)} %shard_map.111), calls=%async_computation.7 | async-start | bytes 2097152 | tf_op jit(solution)/shard_map/all_to_all | solution.py:60
  201.9 28.6 %copy-start.9 = (f32[128,2048]{1,0:T(8,128)}, f32[128,2048]{1,0:T(8,128)S(1)}, u32[]{:S(2)}) copy-start(f32[128,2048]{1,0:T(8,128)S(1)} %collective-permute-done.8.refs_1_) | copy-start | bytes 3145732
  234.3 1.8 collective-permute-start.15
  236.2 7.8 %collective-permute-start.16 = (f32[4,128,128]{2,1,0:T(8,128)S(1)}, f32[4,128,128]{2,1,0:T(8,128)S(1)}, u32[]{:S(2)}, u32[]{:S(2)}) collective-permute-start(f32[4,128,128]{2,1,0:T(8,128)S(1)} %shard_map.113.here_ref), channel_id=1, source_target_pairs={{0,32},{1,33},{2,34},{3,35},{4,36},{5,37},{6,38},{7,39},{8,40},{9,... | collective-permute-start | bytes 786440 | tf_op jit(solution)/shard_map/ppermute | solution.py:67
  291.1 3.9 collective-permute-start.17
  295.0 5.3 %collective-permute-start.18 = (f32[2,128,128]{2,1,0:T(8,128)S(1)}, f32[2,128,128]{2,1,0:T(8,128)S(1)}, u32[]{:S(2)}, u32[]{:S(2)}) collective-permute-start(f32[2,128,128]{2,1,0:T(8,128)S(1)} %shard_map.117.here_ref), channel_id=1, source_target_pairs={{0,1},{1,0},{2,3},{3,2},{4,5},{5,4},{6,7},{7,6},{8,9},{9,8},{10,11... | collective-permute-start | bytes 393224 | tf_op jit(solution)/shard_map/ppermute | solution.py:67
  342.8 4.3 %collective-permute-start.19 = (f32[2,128,128]{2,1,0:T(8,128)S(1)}, f32[2,128,128]{2,1,0:T(8,128)S(1)}, u32[]{:S(2)}, u32[]{:S(2)}) collective-permute-start(f32[2,128,128]{2,1,0:T(8,128)S(1)} %get-tuple-element.74.here_ref), channel_id=1, source_target_pairs={{0,1},{1,0},{2,3},{3,2},{4,5},{5,4},{6,7},{7,6},{8,9},{9,8},{10,11... | collective-permute-start | bytes 393224 | tf_op jit(solution)/shard_map/ppermute | solution.py:67
  375.4 3.9 collective-permute-start.20
  383.1 15.5 %all-to-all-start.14 = ((f32[4,384,128]{2,1,0:T(8,128)}), f32[4,384,128]{2,1,0:T(8,128)S(1)}, u32[]{:S(2)}, u32[]{:S(2)}) async-start(f32[4,384,128]{2,1,0:T(8,128)} %bitcast.34), calls=%async_computation.14 | async-start | bytes 1572864 | tf_op jit(solution)/shard_map/all_to_all | solution.py:60
  401.2 24.0 %all-to-all-start.15 = ((f32[128,16,128]{2,1,0:T(8,128)}), f32[128,16,128]{2,1,0:T(8,128)S(1)}, u32[]{:S(2)}, u32[]{:S(2)}) async-start(f32[128,16,128]{2,1,0:T(8,128)} %bitcast.35), calls=%async_computation.15 | async-start | bytes 2097152 | tf_op jit(solution)/shard_map/all_to_all | solution.py:311

commit v2 on v1

--- a/solution.py
+++ b/solution.py
@@ -95,32 +95,38 @@
     return inward, outward
 
 
-def cut_sends(places, matrices, pieces, index=None, rows=None):
+def cut_sends(places, matrices, pieces, owner=None, rows=None):
     shapes = [(matrices[m].shape[0], matrices[m].shape[1] // (2 * cuts)) for m, cuts, _ in pieces]
     count, total = len(pieces), len(matrices)
-    extra = [] if rows is None else [index[None, :], rows]
+    extra = [] if rows is None else [owner[None, :], rows]
 
     def body(at_ref, *refs):
         sources, refs = refs[:total], refs[total:]
         given, refs = refs[: len(extra)], refs[len(extra) :]
         sends, refs = refs[:count], refs[count:]
-        filled, refs = refs[: len(extra) // 2], refs[len(extra) // 2 :]
+        filled, refs = refs[: len(extra)], refs[len(extra) :]
         stages, sems = refs[:count], refs[count:]
         inward, outward = moves(pieces, at_ref, sources, sends, stages, *sems)
         for group in inward:
             for copy in group:
                 copy.start()
         if extra:
-            slots_body(*given, *filled)
+            slots = filled[0].shape[0]
+            filled[1][...] = slot_of(given[0][...])
+            slots_body(filled[1], given[1], filled[0], 0, slots // 2)
         for group, after in zip(inward, outward):
             for copy in group:
                 copy.wait()
             after.start()
+        if extra:
+            slots_body(filled[1], given[1], filled[0], slots // 2, slots)
         for copy in outward:
             copy.wait()
 
     peers = lax.axis_size("leaf") * lax.axis_size("front")
-    slots = [] if rows is None else [VMEM((peers * SLOTS, rows.shape[1]), F32)]
+    slots = []
+    if extra:
+        slots = [VMEM((peers * SLOTS, rows.shape[1]), F32), VMEM((1, rows.shape[0]), jnp.int32)]
     return pl.pallas_call(
         body,
         in_specs=[pl.BlockSpec(memory_space=pltpu.SMEM)]
@@ -243,9 +249,8 @@
     spread(held_ref, rows_of(solved_ref[...], far_ref[...]), out_ref)
 
 
-def top_body(held_ref, here_ref, there_ref, out_ref):
-    vector = rows_of(*[here_ref[part] + there_ref[part ^ 2] for part in range(4)])
-    spread(held_ref, vector, out_ref)
+def top_body(held_ref, mine_ref, theirs_ref, out_ref):
+    spread(held_ref, rows_of(mine_ref[0], theirs_ref[0], mine_ref[1], theirs_ref[1]), out_ref)
 
 
 def backward_body(held_ref, here_ref, there_ref, solved_ref, out_ref):
@@ -256,9 +261,13 @@
     out_ref[...] = joined(here_ref, there_ref)
 
 
-def core_pair_body(here_ref, there_ref, out_ref):
-    for part in range(4):
-        out_ref[part] = here_ref[part] + there_ref[part ^ 1]
+def add_body(here_ref, there_ref, out_ref):
+    out_ref[...] = here_ref[...] + there_ref[...]
+
+
+def cross_body(here_ref, there_ref, out_ref):
+    for part in range(2):
+        out_ref[part] = here_ref[part] + there_ref[1 - part]
 
 
 def plane_pair_body(here_ref, there_ref, out_ref):
@@ -277,12 +286,23 @@
     out_ref[...] = jnp.broadcast_to(share[None], out_ref.shape)
 
 
-def slots_body(index_ref, rows_ref, out_ref):
+def slot_of(owner):
+    count = owner.shape[1]
+    target = jnp.floor((owner.astype(F32) + 0.5) * (1.0 / count))
+    down = jnp.broadcast_to(target, (8, count)).T[:, :1]
+    earlier = lax.broadcasted_iota(jnp.int32, (count, count), 0) < lax.broadcasted_iota(
+        jnp.int32, (count, count), 1
+    )
+    rank = jnp.sum(jnp.where((down == target) & earlier, 1.0, 0.0), axis=0, keepdims=True)
+    return (target * SLOTS + rank).astype(jnp.int32)
+
+
+def slots_body(index_ref, rows_ref, out_ref, first, last):
     parts = jnp.concatenate(pair_of(rows_ref[...]), axis=1)
     count, width = rows_ref.shape
     index = index_ref[...]
 
-    @pl.loop(0, out_ref.shape[0] // 512)
+    @pl.loop(first // 512, last // 512)
     def _(step):
         start = pl.multiple_of(step * 512, 512)
         slot = lax.broadcasted_iota(jnp.int32, (512, count), 0) + start
@@ -293,7 +313,7 @@
 def to_slots(index, rows):
     peers = lax.axis_size("leaf") * lax.axis_size("front")
     return pl.pallas_call(
-        slots_body,
+        lambda *refs: slots_body(*refs, 0, peers * SLOTS),
         in_specs=vmem_specs(2),
         out_specs=pl.BlockSpec(memory_space=VMEM),
         out_shape=VMEM((peers * SLOTS, rows.shape[1]), F32),
@@ -317,10 +337,6 @@
     row_count, width = app_rhs.shape
     matrices = [m[0, 0] for m in matrices]
 
-    destination = row_owner // row_count
-    send_index = destination * SLOTS + rank_among(
-        destination, jnp.arange(row_count, dtype=jnp.int32)
-    )
     anchor = pivot_source // row_count
     recv_index = anchor * SLOTS + rank_among(anchor, pivot_source)
 
@@ -331,20 +347,17 @@
 
     places = all_places(core, plane)
     first = [(0, 1, 2), (1, 1, 2)]
-    *sends, outgoing = cut_sends(places, matrices[:2], first, send_index, app_rhs)
+    *sends, outgoing, send_index = cut_sends(places, matrices[:2], first, row_owner, app_rhs)
     mats = [[matrices[m], swap(sends[m], CORE)] for m in range(2)]
     ordered = move_rows(outgoing)[recv_index]
     ordered, core, plane = lax.optimization_barrier((ordered, core, plane))
-    late = [(m, 1, 2) for m in range(3)] + [(m, 2, p) for m in (3, 4) for p in (3, 4, 5)]
-    sends = cut_sends(all_places(core, plane), matrices[2:], late)
-    mats += [[matrices[m], swap(sends[m - 2], CORE)] for m in range(2, 5)]
-    mats += [[matrices[m], swap(sends[3 * m - 12], CORE)] for m in (5, 6)]
-    for number, piece in enumerate((4, 5, 7, 8)):
+    late = [(0, 1, 2), (1, 1, 2)] + [(m, 2, p) for m in (2, 3) for p in (4, 5)]
+    sends = cut_sends(all_places(core, plane), matrices[2:4] + matrices[5:], late)
+    mats += [[matrices[m], swap(sends[m - 2], CORE)] for m in (2, 3)]
+    far = []
+    for number, piece in enumerate(range(2, 6)):
         half = swap(sends[piece], (PLANE, PLANE | CORE)[number % 2])
-        mats[5 + number // 2].append(half)
-    inverses = (mats[0], mats[2], mats[4], mats[6])
-    couplings = (mats[1], mats[3], mats[5])
-
+        far.append(half)
     starts = (0, LEAF_PIV, LEAF_PIV + SEP_PIV, LEAF_PIV + 2 * SEP_PIV)
     sizes = (CHIPS, 2 * CHIPS, 4 * CHIPS, 4 * CHIPS)
     own = [ordered[at : at + rows] for at, rows in zip(starts, PIVOTS)]
@@ -352,11 +365,19 @@
     solved = []
     for height in range(3):
         gathered = exchange(tiles, height).reshape(-1, width)
-        here, held = applied(places, inverses[height], gathered, couplings[height])
+        here, held = applied(places, mats[2 * height], gathered, mats[2 * height + 1])
         there = swap(here, CORE)
         outs = [(held.shape[1], width), (2 * PIVOTS[height], width)]
         if height < 2:
             carried, forward = call(forward_body, outs, held, here, there)
+            if height == 0:
+                carried, core, plane = lax.optimization_barrier((carried, core, plane))
+                late = [(0, 1, 2), (1, 2, 3), (2, 2, 3)]
+                sends = cut_sends(all_places(core, plane), matrices[4:], late)
+                for m in range(4, 7):
+                    mats.append([matrices[m], swap(sends[m - 4], CORE)])
+                mats[5] += far[:2]
+                mats[6] += far[2:]
         else:
             (forward,) = call(joined_body, outs[1:], here, there)
             (carried,) = call(plane_body, outs[:1], held, forward, swap(forward, PLANE))
@@ -365,9 +386,11 @@
         (tiles,) = call(
             minus_sum_body, [(sizes[height + 1], SEP_PIV, width)], arrived, own[height + 1]
         )
-    here, held = applied(places, inverses[3], exchange(tiles, 3).reshape(-1, width))
-    (here,) = call(core_pair_body, [here.shape], here, swap(here, CORE))
-    (spread_out,) = call(top_body, [(held.shape[1], width)], held, here, swap(here, PLANE))
+    here, held = applied(places, mats[6], exchange(tiles, 3).reshape(-1, width))
+    mine, theirs = here[0::2], here[1::2]
+    (mine,) = call(add_body, [mine.shape], mine, swap(theirs, CORE))
+    (mine,) = call(cross_body, [mine.shape], mine, swap(mine, PLANE))
+    (spread_out,) = call(top_body, [(held.shape[1], width)], held, mine, swap(mine, CORE))
     pieces = [None, None, None, None]
     for height in (3, 2, 1):
         arrived = exchange(spread_out.reshape(-1, SEP_PIV, width), height)
@@ -375,7 +398,7 @@
             sum_body, [(SEP_PIV, width), (sizes[height], SEP_PIV, width)], arrived
         )
         parent = exchange(tiles, height).reshape(-1, width)
-        here, held = applied(places, couplings[height - 1], parent, inverses[height - 1])
+        here, held = applied(places, mats[2 * height - 1], parent, mats[2 * height - 2])
         if height == 3:
             (here,) = call(plane_pair_body, [(2, SEP_PIV, width)], here, swap(here[2:], PLANE))
         there = swap(here, CORE)
@@ -384,7 +407,7 @@
         )
     pieces[0] = exchange(spread_out.reshape(-1, LEAF_PIV, width), 0).sum(axis=0)
     pivot_order = jnp.concatenate(pieces, axis=0)
-    return move_rows(to_slots(recv_index, pivot_order))[send_index]
+    return move_rows(to_slots(recv_index, pivot_order))[send_index[0]]
 
 
 def solution(mesh):

time: 429 us -> 423 us (0.986)
  waiting for transfers between devices: 182 us -> 175 us
    ppermute x21 -> x22, waiting for transfers between devices: 78.5 us -> 75 us  [swap(): return lax.ppermute(block, AXES, [(i, i ^ mask) for i in range(count)])]
    pallas_call x2 -> x3, Pallas kernels: 13.2 us -> 14.8 us  [cut_sends(): pl.pallas_call(body, in_specs=[pl.BlockSpec(memory_space=pltpu.SMEM)] + [...]
    ppermute x21 -> x22, starting transfers between devices: 23.4 us -> 24.5 us  [swap(): return lax.ppermute(block, AXES, [(i, i ^ mask) for i in range(count)])]
    pallas_call x16 -> x17, Pallas kernels: 21.7 us -> 21.8 us  [call(): pl.pallas_call(body, in_specs=vmem_specs(len(args)), out_specs=vmem_specs...]
  transfers between devices with their start and end apart: 31 -> 32, of which waited for: 21 -> 22; matrix products, arithmetic and copies ran while one was open for 1% -> 1% of each run, Pallas kernels for 3% -> 4%
where the time goes in v2:
time: 423 us; the launch traced here: 422 us
  waiting for transfers between devices  175 us (41%)
  blocking collectives  101 us (24%)
  starting transfers between devices  71.4 us (17%)
  Pallas kernels  65.2 us (15%)
  local copies, waits for them, and re-layouts  8.48 us (2%)
    all_to_all x6, blocking collectives, exchange(): lax.all_to_all(tiles, AXES, 0, 0, axis_index_groups=same_core_groups(min(...  101 us
    ppermute x22, waiting for transfers between devices, swap(): return lax.ppermute(block, AXES, [(i, i ^ mask) for i in range(count)])  75 us
    all_to_all x8, waiting for transfers between devices, exchange(): lax.all_to_all(tiles, AXES, 0, 0, axis_index_groups=same_core_groups(min(...  62.9 us
    all_to_all x2, waiting for transfers between devices, move_rows(): return lax.all_to_all(tiles, AXES, 0, 0, tiled=True).reshape(outgoing.shape)  36.8 us
    all_to_all x8, starting transfers between devices, exchange(): lax.all_to_all(tiles, AXES, 0, 0, axis_index_groups=same_core_groups(min(...  32 us
    pallas_call x7, Pallas kernels, applied(): pl.pallas_call(body, in_specs=[pl.BlockSpec(memory_space=pltpu.SMEM)] + [...  26.1 us
    ppermute x22, starting transfers between devices, swap(): return lax.ppermute(block, AXES, [(i, i ^ mask) for i in range(count)])  24.5 us
    pallas_call x17, Pallas kernels, call(): pl.pallas_call(body, in_specs=vmem_specs(len(args)), out_specs=vmem_specs...  21.8 us
  transfers between devices with their start and end apart: 32, of which 22 were waited for; matrix products, arithmetic and copies ran while one was open for 1% of the time, Pallas kernels for 4%

profile of v2, /device:TPU:1, one launch (start us, length us, event | category | flops | bytes accessed | tf_op | source)
XLA Modules:
  0.0 421.8 jit_solution(12713266783025540996)
XLA Ops:
  1.8 5.1 %shard_map.100 = (f32[384,1536]{1,0:T(8,128)}, f32[384,1024]{1,0:T(8,128)}, f32[2048,128]{1,0:T(8,128)}, s32[1,768]{1,0:T(1,128)S(1)}) custom-call(s32[6]{0:T(128)S(1)} %stack.69.at_ref, f32[384,3072]{1,0:T(8,128)} %bitcast.59, f32[384,2048]{1,0:T(8,128)} %bitcast.65, s32[1,768]{1,0:T(1,128)S(1)} %broadcast_in_dim.9.refs_2_, f32[768,128]{1,0:T(8,128)S(1)} %copy-done.2), custom_call_target="tpu_custom_call" | custom-call | tf_op jit(solution)/shard_map/pallas_call | solution.py:130
  6.9 1.5 collective-permute-start.1
  8.4 10.2 %all-to-all-start = ((f32[128,16,128]{2,1,0:T(8,128)}), f32[128,16,128]{2,1,0:T(8,128)S(1)}, u32[]{:S(2)}, u32[]{:S(2)}) async-start(f32[128,16,128]{2,1,0:T(8,128)} %bitcast.9), calls=%async_computation | async-start | bytes 2097152 | tf_op jit(solution)/shard_map/all_to_all | solution.py:331
  18.6 1.1 collective-permute-start
  20.3 17.5 %all-to-all-done = f32[128,16,128]{2,1,0:T(8,128)S(1)} async-done(((f32[128,16,128]{2,1,0:T(8,128)}), f32[128,16,128]{2,1,0:T(8,128)S(1)}, u32[]{:S(2)}, u32[]{:S(2)}) %all-to-all-start) | async-done | bytes 1048608 | tf_op jit(solution)/shard_map/all_to_all | solution.py:331
  37.8 1.6 gather_fusion
  40.4 3.5 all-to-all-start.1
  43.9 11.4 %all-to-all-done.1 = f32[4,384,128]{2,1,0:T(8,128)S(1)} async-done(((f32[4,384,128]{2,1,0:T(8,128)}), f32[4,384,128]{2,1,0:T(8,128)S(1)}, u32[]{:S(2)}, u32[]{:S(2)}) %all-to-all-start.1) | async-done | bytes 786464 | tf_op jit(solution)/shard_map/all_to_all | solution.py:60
  55.3 4.5 %shard_map.102 = (f32[2,384,128]{2,1,0:T(8,128)S(1)}, f32[768,1024]{1,0:T(8,128)S(1)}) custom-call(s32[6]{0:T(128)S(1)} %stack.69.at_ref, f32[384,3072]{1,0:T(8,128)} %bitcast.60, f32[384,1536]{1,0:T(8,128)} %collective-permute-done.1.refs_1_.refs_3_, f32[384,2048]{1,0:T(8,128)} %bitcast.66, f32[384,1024]{1,0:T(8,128)} %copy-done.3, f32[1536,128]{1,0:T(8,128)S(1)} %bitcast.51), custom_call_target="tpu_custom_call" | custom-call | tf_op jit(solution)/shard_map/pallas_call | solution.py:205
  59.8 1.6 copy-done
  61.4 1.8 collective-permute-start.4
  63.3 6.2 %shard_map.101 = (f32[128,1024]{1,0:T(8,128)}, f32[128,2048]{1,0:T(8,128)}, f32[128,2048]{1,0:T(8,128)}, f32[128,2048]{1,0:T(8,128)}, f32[128,2048]{1,0:T(8,128)}, /*index=5*/f32[128,2048]{1,0:T(8,128)}) custom-call(s32[6]{0:T(128)S(1)} %stack.76.at_ref, f32[128,2048]{1,0:T(8,128)} %bitcast.76, f32[128,4096]{1,0:T(8,128)} %bitcast.68, f32[128,8192]{1,0:T(8,128)} %bitcast.55, ...), custom_call_target="tpu_custom_call" | custom-call | tf_op jit(solution)/shard_map/pallas_call | solution.py:130
  69.6 2.8 shard_map.103
  72.4 3.5 all-to-all-start.2
  76.5 8.5 %all-to-all-done.2.tiles_ref = f32[8,128,128]{2,1,0:T(8,128)S(1)} async-done(((f32[8,128,128]{2,1,0:T(8,128)}), f32[8,128,128]{2,1,0:T(8,128)S(1)}, u32[]{:S(2)}, u32[]{:S(2)}) %all-to-all-start.2) | async-done | bytes 524320 | tf_op jit(solution)/shard_map/all_to_all | solution.py:60
  85.8 3.5 all-to-all-start.3
  89.3 8.5 %all-to-all-done.3 = f32[8,128,128]{2,1,0:T(8,128)S(1)} async-done(((f32[8,128,128]{2,1,0:T(8,128)}), f32[8,128,128]{2,1,0:T(8,128)S(1)}, u32[]{:S(2)}, u32[]{:S(2)}) %all-to-all-start.3) | async-done | bytes 524320 | tf_op jit(solution)/shard_map/all_to_all | solution.py:60
  97.8 2.8 shard_map.106
  100.6 1.9 collective-permute-start.12
  103.5 2.8 shard_map.107
  106.2 3.7 all-to-all-start.4
  110.0 2.0 collective-permute-start.7
  112.1 3.5 shard_map.104
  116.2 10.2 %all-to-all-done.4.tiles_ref = f32[16,128,128]{2,1,0:T(8,128)S(1)} async-done(((f32[16,128,128]{2,1,0:T(8,128)}), f32[16,128,128]{2,1,0:T(8,128)S(1)}, u32[]{:S(2)}, u32[]{:S(2)}) %all-to-all-start.4) | async-done | bytes 1048608 | tf_op jit(solution)/shard_map/all_to_all | solution.py:60
  127.4 4.0 all-to-all-start.5
  131.5 3.1 collective-permute-done.6.refs_4_.refs_2_
  134.6 23.1 %collective-permute-done.7.refs_5_.refs_3_ = f32[128,2048]{1,0:T(8,128)} collective-permute-done((f32[128,2048]{1,0:T(8,128)}, f32[128,2048]{1,0:T(8,128)}, u32[]{:S(2)}, u32[]{:S(2)}) %collective-permute-start.7) | collective-permute-done | bytes 1048608 | tf_op jit(solution)/shard_map/ppermute | solution.py:67
  157.7 3.9 shard_map.109
  161.6 1.3 collective-permute-done.13.there_ref
  163.1 4.9 %collective-permute-done.14.far_ref = f32[256,128]{1,0:T(8,128)S(1)} collective-permute-done((f32[256,128]{1,0:T(8,128)S(1)}, f32[256,128]{1,0:T(8,128)S(1)}, u32[]{:S(2)}, u32[]{:S(2)}) %collective-permute-start.14) | collective-permute-done | bytes 131104 | tf_op jit(solution)/shard_map/ppermute | solution.py:67
  168.0 3.4 shard_map.111
  171.4 6.5 %all-to-all-start.6 = ((f32[16,128,128]{2,1,0:T(8,128)}), f32[16,128,128]{2,1,0:T(8,128)S(1)}, u32[]{:S(2)}, u32[]{:S(2)}) async-start(f32[16,128,128]{2,1,0:T(8,128)} %bitcast.32), calls=%async_computation.6 | async-start | bytes 2097152 | tf_op jit(solution)/shard_map/all_to_all | solution.py:60
  178.0 2.9 collective-permute-start.11
  180.9 12.4 %all-to-all-done.6.tiles_ref = f32[16,128,128]{2,1,0:T(8,128)S(1)} async-done(((f32[16,128,128]{2,1,0:T(8,128)}), f32[16,128,128]{2,1,0:T(8,128)S(1)}, u32[]{:S(2)}, u32[]{:S(2)}) %all-to-all-start.6) | async-done | bytes 1048608 | tf_op jit(solution)/shard_map/all_to_all | solution.py:60
  194.5 3.9 all-to-all-start.7
  198.4 3.3 collective-permute-done.10.refs_2_
  201.6 24.0 %collective-permute-done.11.refs_3_ = f32[128,2048]{1,0:T(8,128)} collective-permute-done((f32[128,2048]{1,0:T(8,128)}, f32[128,2048]{1,0:T(8,128)}, u32[]{:S(2)}, u32[]{:S(2)}) %collective-permute-start.11) | collective-permute-done | bytes 1048608 | tf_op jit(solution)/shard_map/ppermute | solution.py:67
  225.7 3.8 shard_map.113
  229.5 1.3 collective-permute-done.15.there_ref
  231.0 4.9 %collective-permute-done.16.there_ref = f32[2,128,128]{2,1,0:T(8,128)S(1)} collective-permute-done((f32[2,128,128]{2,1,0:T(8,128)S(1)}, f32[2,128,128]{2,1,0:T(8,128)S(1)}, u32[]{:S(2)}, u32[]{:S(2)}) %collective-permute-start.16) | collective-permute-done | bytes 131104 | tf_op jit(solution)/shard_map/ppermute | solution.py:67
  238.0 2.4 shard_map.116
  240.4 22.4 %all_to_all.80.tiles_ref = f32[16,128,128]{2,1,0:T(8,128)S(1)} all-to-all(f32[16,128,128]{2,1,0:T(8,128)S(1)} %bitcast.50), channel_id=1, replica_groups={{0,8,16,24,2,10,18,26,4,12,20,28,6,14,22,30},{1,9,17,25,3,11,19,27,5,13..., dimensions={0} | all-to-all | bytes 2097152 | tf_op jit(solution)/shard_map/all_to_all | solution.py:60
  262.9 18.3 %all_to_all.81 = f32[16,128,128]{2,1,0:T(8,128)S(1)} all-to-all(f32[16,128,128]{2,1,0:T(8,128)S(1)} %get-tuple-element.76), channel_id=1, replica_groups={{0,8,16,24,2,10,18,26,4,12,20,28,6,14,22,30},{1,9,17,25,3,11,19,27,5,13..., dimensions={0} | all-to-all | bytes 2097152 | tf_op jit(solution)/shard_map/all_to_all | solution.py:60
  281.2 3.9 shard_map.118
  285.3 3.8 collective-permute-done.18.there_ref
  289.1 4.5 %collective-permute-start.19 = (f32[2,128,128]{2,1,0:T(8,128)S(1)}, f32[2,128,128]{2,1,0:T(8,128)S(1)}, u32[]{:S(2)}, u32[]{:S(2)}) collective-permute-start(f32[2,128,128]{2,1,0:T(8,128)S(1)} %shard_map.119.here_ref), channel_id=1, source_target_pairs={{0,1},{1,0},{2,3},{3,2},{4,5},{5,4},{6,7},{7,6},{8,9},{9,8},{10,11... | collective-permute-start | bytes 393224 | tf_op jit(solution)/shard_map/ppermute | solution.py:67
  294.6 1.8 shard_map.120
  296.4 19.0 %all_to_all.82.tiles_ref = f32[16,128,128]{2,1,0:T(8,128)S(1)} all-to-all(f32[16,128,128]{2,1,0:T(8,128)S(1)} %bitcast.48), channel_id=1, replica_groups={{0,8,16,24,2,10,18,26,4,12,20,28,6,14,22,30},{1,9,17,25,3,11,19,27,5,13..., dimensions={0} | all-to-all | bytes 2097152 | tf_op jit(solution)/shard_map/all_to_all | solution.py:60
  315.5 18.3 %all_to_all.83 = f32[16,128,128]{2,1,0:T(8,128)S(1)} all-to-all(f32[16,128,128]{2,1,0:T(8,128)S(1)} %get-tuple-element.79), channel_id=1, replica_groups={{0,8,16,24,2,10,18,26,4,12,20,28,6,14,22,30},{1,9,17,25,3,11,19,27,5,13..., dimensions={0} | all-to-all | bytes 2097152 | tf_op jit(solution)/shard_map/all_to_all | solution.py:60
  333.9 3.1 shard_map.122
  337.0 3.3 collective-permute-start.20
  341.3 1.3 shard_map.123
  342.6 11.7 %all_to_all.84.tiles_ref = f32[8,128,128]{2,1,0:T(8,128)S(1)} all-to-all(f32[8,128,128]{2,1,0:T(8,128)S(1)} %bitcast.53), channel_id=1, replica_groups={{0,8,2,10,4,12,6,14},{1,9,3,11,5,13,7,15},{16,24,18,26,20,28,22,30},{17..., dimensions={0} | all-to-all | bytes 1048576 | tf_op jit(solution)/shard_map/all_to_all | solution.py:60
  354.4 11.0 %all_to_all.85 = f32[8,128,128]{2,1,0:T(8,128)S(1)} all-to-all(f32[8,128,128]{2,1,0:T(8,128)S(1)} %get-tuple-element.83), channel_id=1, replica_groups={{0,8,2,10,4,12,6,14},{1,9,3,11,5,13,7,15},{16,24,18,26,20,28,22,30},{17..., dimensions={0} | all-to-all | bytes 1048576 | tf_op jit(solution)/shard_map/all_to_all | solution.py:60
  365.3 4.2 shard_map.125
  369.5 2.5 collective-permute-start.21
  372.1 1.3 collective-permute-done.21.there_ref
  373.4 3.9 shard_map.126
  377.3 3.5 all-to-all-start.14
  380.8 12.0 %all-to-all-done.14 = f32[4,384,128]{2,1,0:T(8,128)S(1)} async-done(((f32[4,384,128]{2,1,0:T(8,128)}), f32[4,384,128]{2,1,0:T(8,128)S(1)}, u32[]{:S(2)}, u32[]{:S(2)}) %all-to-all-start.14) | async-done | bytes 786464 | tf_op jit(solution)/shard_map/all_to_all | solution.py:60
  392.8 2.6 shard_map.127
  395.5 4.7 %all-to-all-start.15 = ((f32[128,16,128]{2,1,0:T(8,128)}), f32[128,16,128]{2,1,0:T(8,128)S(1)}, u32[]{:S(2)}, u32[]{:S(2)}) async-start(f32[128,16,128]{2,1,0:T(8,128)} %bitcast.41), calls=%async_computation.15 | async-start | bytes 2097152 | tf_op jit(solution)/shard_map/all_to_all | solution.py:331
  400.2 19.3 %all-to-all-done.15 = f32[128,16,128]{2,1,0:T(8,128)S(1)} async-done(((f32[128,16,128]{2,1,0:T(8,128)}), f32[128,16,128]{2,1,0:T(8,128)S(1)}, u32[]{:S(2)}, u32[]{:S(2)}) %all-to-all-start.15) | async-done | bytes 1048608 | tf_op jit(solution)/shard_map/all_to_all | solution.py:331
  419.5 2.3 gather_fusion.1
  (76 shorter events, 14.0 us)
Async XLA Ops:
  0.8 1.0 copy-start.2
  1.8 18.0 %copy-start.10 = (s32[768]{0:T(1024)S(1)}, s32[768]{0:T(1024)}, u32[]{:S(2)}) copy-start(s32[768]{0:T(1024)} %param.11) | copy-start | bytes 9220
  6.9 48.4 %collective-permute-start.1 = (f32[384,1536]{1,0:T(8,128)}, f32[384,1536]{1,0:T(8,128)}, u32[]{:S(2)}, u32[]{:S(2)}) collective-permute-start(f32[384,1536]{1,0:T(8,128)} %get-tuple-element.49), channel_id=1, source_target_pairs={{0,1},{1,0},{2,3},{3,2},{4,5},{5,4},{6,7},{7,6},{8,9},{9,8},{10,11... | collective-permute-start | bytes 7077896 | tf_op jit(solution)/shard_map/ppermute | solution.py:67
  8.4 29.5 %all-to-all-start = ((f32[128,16,128]{2,1,0:T(8,128)}), f32[128,16,128]{2,1,0:T(8,128)S(1)}, u32[]{:S(2)}, u32[]{:S(2)}) async-start(f32[128,16,128]{2,1,0:T(8,128)} %bitcast.9), calls=%async_computation | async-start | bytes 2097152 | tf_op jit(solution)/shard_map/all_to_all | solution.py:331
  18.6 25.3 %collective-permute-start = (f32[384,1024]{1,0:T(8,128)}, f32[384,1024]{1,0:T(8,128)S(1)}, u32[]{:S(2)}, u32[]{:S(2)}) collective-permute-start(f32[384,1024]{1,0:T(8,128)} %get-tuple-element.48), channel_id=1, source_target_pairs={{0,1},{1,0},{2,3},{3,2},{4,5},{5,4},{6,7},{7,6},{8,9},{9,8},{10,11... | collective-permute-start | bytes 4718600 | tf_op jit(solution)/shard_map/ppermute | solution.py:67
  39.4 20.4 %copy-start.7 = (f32[768,128]{1,0:T(8,128)}, f32[768,128]{1,0:T(8,128)S(1)}, u32[]{:S(2)}) copy-start(f32[768,128]{1,0:T(8,128)S(1)} %gather_fusion) | copy-start | bytes 1179652
  40.4 14.9 %all-to-all-start.1 = ((f32[4,384,128]{2,1,0:T(8,128)}), f32[4,384,128]{2,1,0:T(8,128)S(1)}, u32[]{:S(2)}, u32[]{:S(2)}) async-start(f32[4,384,128]{2,1,0:T(8,128)} %broadcast_in_dim.11), calls=%async_computation.1 | async-start | bytes 1572864 | tf_op jit(solution)/shard_map/all_to_all | solution.py:60
  43.9 11.4 %copy-start.3 = (f32[384,1024]{1,0:T(8,128)}, f32[384,1024]{1,0:T(8,128)S(1)}, u32[]{:S(2)}) copy-start(f32[384,1024]{1,0:T(8,128)S(1)} %collective-permute-done.refs_3_.refs_1_) | copy-start | bytes 4718596
  59.8 1.6 copy-start
  61.4 8.2 %collective-permute-start.4 = (f32[2,384,128]{2,1,0:T(8,128)S(1)}, f32[2,384,128]{2,1,0:T(8,128)S(1)}, u32[]{:S(2)}, u32[]{:S(2)}) collective-permute-start(f32[2,384,128]{2,1,0:T(8,128)S(1)} %get-tuple-element.57.here_ref), channel_id=1, source_target_pairs={{0,1},{1,0},{2,3},{3,2},{4,5},{5,4},{6,7},{7,6},{8,9},{9,8},{10,11... | collective-permute-start | bytes 1179656 | tf_op jit(solution)/shard_map/ppermute | solution.py:67
  63.3 6.3 %copy-start.1 = (f32[768,1024]{1,0:T(8,128)S(1)}, f32[768,1024]{1,0:T(8,128)}, u32[]{:S(2)}) copy-start(f32[768,1024]{1,0:T(8,128)} %copy-done) | copy-start | bytes 9437188
  69.5 19.8 %collective-permute-start.2 = (f32[128,2048]{1,0:T(8,128)}, f32[128,2048]{1,0:T(8,128)S(1)}, u32[]{:S(2)}, u32[]{:S(2)}) collective-permute-start(f32[128,2048]{1,0:T(8,128)} %get-tuple-element.53), channel_id=1, source_target_pairs={{0,1},{1,0},{2,3},{3,2},{4,5},{5,4},{6,7},{7,6},{8,9},{9,8},{10,11... | collective-permute-start | bytes 3145736 | tf_op jit(solution)/shard_map/ppermute | solution.py:67
  69.6 6.8 %copy-start.8 = (f32[768,128]{1,0:T(8,128)S(1)}, f32[768,128]{1,0:T(8,128)}, u32[]{:S(2)}) copy-start(f32[768,128]{1,0:T(8,128)} %copy-done.7) | copy-start | bytes 1179652
  72.4 12.6 %all-to-all-start.2 = ((f32[8,128,128]{2,1,0:T(8,128)}), f32[8,128,128]{2,1,0:T(8,128)S(1)}, u32[]{:S(2)}, u32[]{:S(2)}) async-start(f32[8,128,128]{2,1,0:T(8,128)} %bitcast.28), calls=%async_computation.2 | async-start | bytes 1048576 | tf_op jit(solution)/shard_map/all_to_all | solution.py:60
  75.9 13.4 %collective-permute-start.3 = (f32[128,1024]{1,0:T(8,128)}, f32[128,1024]{1,0:T(8,128)S(1)}, u32[]{:S(2)}, u32[]{:S(2)}) collective-permute-start(f32[128,1024]{1,0:T(8,128)} %get-tuple-element.54), channel_id=1, source_target_pairs={{0,1},{1,0},{2,3},{3,2},{4,5},{5,4},{6,7},{7,6},{8,9},{9,8},{10,11... | collective-permute-start | bytes 1572872 | tf_op jit(solution)/shard_map/ppermute | solution.py:67
  85.8 12.0 %all-to-all-start.3 = ((f32[8,128,128]{2,1,0:T(8,128)}), f32[8,128,128]{2,1,0:T(8,128)S(1)}, u32[]{:S(2)}, u32[]{:S(2)}) async-start(f32[8,128,128]{2,1,0:T(8,128)} %shard_map.105), calls=%async_computation.3 | async-start | bytes 1048576 | tf_op jit(solution)/shard_map/all_to_all | solution.py:60
  89.3 8.5 %copy-start.6 = (f32[128,1024]{1,0:T(8,128)}, f32[128,1024]{1,0:T(8,128)S(1)}, u32[]{:S(2)}) copy-start(f32[128,1024]{1,0:T(8,128)S(1)} %collective-permute-done.3.refs_1_.refs_3_) | copy-start | bytes 1572868
  89.3 8.5 %copy-start.5 = (f32[128,2048]{1,0:T(8,128)}, f32[128,2048]{1,0:T(8,128)S(1)}, u32[]{:S(2)}) copy-start(f32[128,2048]{1,0:T(8,128)S(1)} %collective-permute-done.2.refs_3_.refs_1_) | copy-start | bytes 3145732
  100.6 2.9 collective-permute-start.12
  106.2 20.1 %all-to-all-start.4 = ((f32[16,128,128]{2,1,0:T(8,128)}), f32[16,128,128]{2,1,0:T(8,128)S(1)}, u32[]{:S(2)}, u32[]{:S(2)}) async-start(f32[16,128,128]{2,1,0:T(8,128)} %bitcast.30), calls=%async_computation.4 | async-start | bytes 2097152 | tf_op jit(solution)/shard_map/all_to_all | solution.py:60
  109.9 24.6 %collective-permute-start.6 = (f32[128,2048]{1,0:T(8,128)}, f32[128,2048]{1,0:T(8,128)S(1)}, u32[]{:S(2)}, u32[]{:S(2)}) collective-permute-start(f32[128,2048]{1,0:T(8,128)} %get-tuple-element.62), channel_id=1, source_target_pairs={{0,32},{1,33},{2,34},{3,35},{4,36},{5,37},{6,38},{7,39},{8,40},{9,... | collective-permute-start | bytes 3145736 | tf_op jit(solution)/shard_map/ppermute | solution.py:67
  110.0 47.7 %collective-permute-start.7 = (f32[128,2048]{1,0:T(8,128)}, f32[128,2048]{1,0:T(8,128)}, u32[]{:S(2)}, u32[]{:S(2)}) collective-permute-start(f32[128,2048]{1,0:T(8,128)} %get-tuple-element.63), channel_id=1, source_target_pairs={{0,33},{1,32},{2,35},{3,34},{4,37},{5,36},{6,39},{7,38},{8,41},{9,... | collective-permute-start | bytes 3145736 | tf_op jit(solution)/shard_map/ppermute | solution.py:67
  115.6 42.1 %collective-permute-start.8 = (f32[128,2048]{1,0:T(8,128)}, f32[128,2048]{1,0:T(8,128)}, u32[]{:S(2)}, u32[]{:S(2)}) collective-permute-start(f32[128,2048]{1,0:T(8,128)} %get-tuple-element.64), channel_id=1, source_target_pairs={{0,1},{1,0},{2,3},{3,2},{4,5},{5,4},{6,7},{7,6},{8,9},{9,8},{10,11... | collective-permute-start | bytes 3145736 | tf_op jit(solution)/shard_map/ppermute | solution.py:67
  115.7 42.0 %collective-permute-start.5 = (f32[128,2048]{1,0:T(8,128)}, f32[128,2048]{1,0:T(8,128)}, u32[]{:S(2)}, u32[]{:S(2)}) collective-permute-start(f32[128,2048]{1,0:T(8,128)} %get-tuple-element.61), channel_id=1, source_target_pairs={{0,1},{1,0},{2,3},{3,2},{4,5},{5,4},{6,7},{7,6},{8,9},{9,8},{10,11... | collective-permute-start | bytes 3145736 | tf_op jit(solution)/shard_map/ppermute | solution.py:67
  127.4 30.2 %all-to-all-start.5 = ((f32[16,128,128]{2,1,0:T(8,128)}), f32[16,128,128]{2,1,0:T(8,128)S(1)}, u32[]{:S(2)}, u32[]{:S(2)}) async-start(f32[16,128,128]{2,1,0:T(8,128)} %shard_map.108), calls=%async_computation.5 | async-start | bytes 2097152 | tf_op jit(solution)/shard_map/all_to_all | solution.py:60
  134.6 23.1 %copy-start.4 = (f32[128,2048]{1,0:T(8,128)}, f32[128,2048]{1,0:T(8,128)S(1)}, u32[]{:S(2)}) copy-start(f32[128,2048]{1,0:T(8,128)S(1)} %collective-permute-done.6.refs_4_.refs_2_) | copy-start | bytes 3145732
  161.6 1.4 collective-permute-start.13
  163.0 5.0 %collective-permute-start.14 = (f32[256,128]{1,0:T(8,128)S(1)}, f32[256,128]{1,0:T(8,128)S(1)}, u32[]{:S(2)}, u32[]{:S(2)}) collective-permute-start(f32[256,128]{1,0:T(8,128)S(1)} %shard_map.110.solved_ref), channel_id=1, source_target_pairs={{0,32},{1,33},{2,34},{3,35},{4,36},{5,37},{6,38},{7,39},{8,40},{9,... | collective-permute-start | bytes 393224 | tf_op jit(solution)/shard_map/ppermute | solution.py:67
  171.4 21.9 %all-to-all-start.6 = ((f32[16,128,128]{2,1,0:T(8,128)}), f32[16,128,128]{2,1,0:T(8,128)S(1)}, u32[]{:S(2)}, u32[]{:S(2)}) async-start(f32[16,128,128]{2,1,0:T(8,128)} %bitcast.32), calls=%async_computation.6 | async-start | bytes 2097152 | tf_op jit(solution)/shard_map/all_to_all | solution.py:60
  177.9 23.7 %collective-permute-start.10 = (f32[128,2048]{1,0:T(8,128)}, f32[128,2048]{1,0:T(8,128)S(1)}, u32[]{:S(2)}, u32[]{:S(2)}) collective-permute-start(f32[128,2048]{1,0:T(8,128)} %get-tuple-element.66), channel_id=1, source_target_pairs={{0,32},{1,33},{2,34},{3,35},{4,36},{5,37},{6,38},{7,39},{8,40},{9,... | collective-permute-start | bytes 3145736 | tf_op jit(solution)/shard_map/ppermute | solution.py:67
  178.0 47.7 %collective-permute-start.11 = (f32[128,2048]{1,0:T(8,128)}, f32[128,2048]{1,0:T(8,128)}, u32[]{:S(2)}, u32[]{:S(2)}) collective-permute-start(f32[128,2048]{1,0:T(8,128)} %get-tuple-element.67), channel_id=1, source_target_pairs={{0,33},{1,32},{2,35},{3,34},{4,37},{5,36},{6,39},{7,38},{8,41},{9,... | collective-permute-start | bytes 3145736 | tf_op jit(solution)/shard_map/ppermute | solution.py:67
  180.9 44.8 %collective-permute-start.9 = (f32[128,2048]{1,0:T(8,128)}, f32[128,2048]{1,0:T(8,128)}, u32[]{:S(2)}, u32[]{:S(2)}) collective-permute-start(f32[128,2048]{1,0:T(8,128)} %get-tuple-element.65), channel_id=1, source_target_pairs={{0,1},{1,0},{2,3},{3,2},{4,5},{5,4},{6,7},{7,6},{8,9},{9,8},{10,11... | collective-permute-start | bytes 3145736 | tf_op jit(solution)/shard_map/ppermute | solution.py:67
  194.5 31.2 %all-to-all-start.7 = ((f32[16,128,128]{2,1,0:T(8,128)}), f32[16,128,128]{2,1,0:T(8,128)S(1)}, u32[]{:S(2)}, u32[]{:S(2)}) async-start(f32[16,128,128]{2,1,0:T(8,128)} %shard_map.112), calls=%async_computation.7 | async-start | bytes 2097152 | tf_op jit(solution)/shard_map/all_to_all | solution.py:60
  201.6 24.0 %copy-start.9 = (f32[128,2048]{1,0:T(8,128)}, f32[128,2048]{1,0:T(8,128)S(1)}, u32[]{:S(2)}) copy-start(f32[128,2048]{1,0:T(8,128)S(1)} %collective-permute-done.10.refs_2_) | copy-start | bytes 3145732
  229.5 1.4 collective-permute-start.15
  230.9 5.0 %collective-permute-start.16 = (f32[2,128,128]{2,1,0:T(8,128)S(1)}, f32[2,128,128]{2,1,0:T(8,128)S(1)}, u32[]{:S(2)}, u32[]{:S(2)}) collective-permute-start(f32[2,128,128]{2,1,0:T(8,128)S(1)} %shard_map.114.here_ref), channel_id=1, source_target_pairs={{0,32},{1,33},{2,34},{3,35},{4,36},{5,37},{6,38},{7,39},{8,40},{9,... | collective-permute-start | bytes 393224 | tf_op jit(solution)/shard_map/ppermute | solution.py:67
  235.9 2.1 collective-permute-start.17
  285.2 3.9 collective-permute-start.18
  289.1 5.5 %collective-permute-start.19 = (f32[2,128,128]{2,1,0:T(8,128)S(1)}, f32[2,128,128]{2,1,0:T(8,128)S(1)}, u32[]{:S(2)}, u32[]{:S(2)}) collective-permute-start(f32[2,128,128]{2,1,0:T(8,128)S(1)} %shard_map.119.here_ref), channel_id=1, source_target_pairs={{0,1},{1,0},{2,3},{3,2},{4,5},{5,4},{6,7},{7,6},{8,9},{9,8},{10,11... | collective-permute-start | bytes 393224 | tf_op jit(solution)/shard_map/ppermute | solution.py:67
  337.0 4.3 %collective-permute-start.20 = (f32[2,128,128]{2,1,0:T(8,128)S(1)}, f32[2,128,128]{2,1,0:T(8,128)S(1)}, u32[]{:S(2)}, u32[]{:S(2)}) collective-permute-start(f32[2,128,128]{2,1,0:T(8,128)S(1)} %get-tuple-element.81.here_ref), channel_id=1, source_target_pairs={{0,1},{1,0},{2,3},{3,2},{4,5},{5,4},{6,7},{7,6},{8,9},{9,8},{10,11... | collective-permute-start | bytes 393224 | tf_op jit(solution)/shard_map/ppermute | solution.py:67
  369.5 3.9 collective-permute-start.21
  377.3 15.5 %all-to-all-start.14 = ((f32[4,384,128]{2,1,0:T(8,128)}), f32[4,384,128]{2,1,0:T(8,128)S(1)}, u32[]{:S(2)}, u32[]{:S(2)}) async-start(f32[4,384,128]{2,1,0:T(8,128)} %bitcast.40), calls=%async_computation.14 | async-start | bytes 1572864 | tf_op jit(solution)/shard_map/all_to_all | solution.py:60
  395.5 24.0 %all-to-all-start.15 = ((f32[128,16,128]{2,1,0:T(8,128)}), f32[128,16,128]{2,1,0:T(8,128)S(1)}, u32[]{:S(2)}, u32[]{:S(2)}) async-start(f32[128,16,128]{2,1,0:T(8,128)} %bitcast.41), calls=%async_computation.15 | async-start | bytes 2097152 | tf_op jit(solution)/shard_map/all_to_all | solution.py:331

commit v3 on v2

--- a/solution.py
+++ b/solution.py
@@ -255,6 +255,35 @@
 
 def backward_body(held_ref, here_ref, there_ref, solved_ref, out_ref):
     spread(held_ref, solved_ref[...] - joined(here_ref, there_ref), out_ref)
+
+
+def leaf_body(chip_ref, held_ref, here_ref, there_ref, solved_ref, *outs):
+    vector = solved_ref[...] - joined(here_ref, there_ref)
+    left = jnp.concatenate(pair_of(vector.T), axis=0)
+    count, width = vector.shape[1], held_ref.shape[1] // CHIPS
+    for turn, out_ref in enumerate(outs):
+        block = lax.rem(chip_ref[0] + turn, CHIPS)
+        up, down = pair_of(held_ref[:, pl.ds(pl.multiple_of(block * width, 128), width)])
+        full = dot(left, up) + dot(left, down)
+        out_ref[...] = (full[:count] + full[count:]).T
+
+
+def leaf_sum(chip, held, here, there, solved):
+    shape = (held.shape[1] // CHIPS, here.shape[2])
+    parts = pl.pallas_call(
+        leaf_body,
+        in_specs=[pl.BlockSpec(memory_space=pltpu.SMEM)] + vmem_specs(4),
+        out_specs=vmem_specs(CHIPS),
+        out_shape=[VMEM(shape, F32)] * CHIPS,
+        compiler_params=params(16),
+    )(chip.reshape(1), *[on_chip(a) for a in (held, here, there, solved)])
+    fronts = lax.axis_size("front")
+    count = lax.axis_size("leaf") * fronts
+    total = parts[0]
+    for turn in (1, 3, 2):
+        route = [(i, i - i % fronts + (i + 2 * turn) % fronts) for i in range(count)]
+        total = total + lax.ppermute(parts[turn], AXES, route)
+    return total
 
 
 def joined_body(here_ref, there_ref, out_ref):
@@ -402,10 +431,11 @@
         if height == 3:
             (here,) = call(plane_pair_body, [(2, SEP_PIV, width)], here, swap(here[2:], PLANE))
         there = swap(here, CORE)
-        (spread_out,) = call(
-            backward_body, [(held.shape[1], width)], held, here, there, solved[height - 1]
-        )
-    pieces[0] = exchange(spread_out.reshape(-1, LEAF_PIV, width), 0).sum(axis=0)
+        if height > 1:
+            outs = [(held.shape[1], width)]
+            (spread_out,) = call(backward_body, outs, held, here, there, solved[height - 1])
+    chip = lax.axis_index("front") // 2
+    pieces[0] = leaf_sum(chip, held, here, there, solved[0])
     pivot_order = jnp.concatenate(pieces, axis=0)
     return move_rows(to_slots(recv_index, pivot_order))[send_index[0]]
 

time: 423 us -> 423 us (level)
  local copies, waits for them, and re-layouts: 8.48 us -> 13 us
    all_to_all x8 -> x7, waiting for transfers between devices: 62.9 us -> 51 us  [exchange(): lax.all_to_all(tiles, AXES, 0, 0, axis_index_groups=same_core_groups(min(...]
    ppermute x0 -> x3, waiting for transfers between devices: none -> 8.27 us  [leaf_sum(): total = total + lax.ppermute(parts[turn], AXES, route)]
    unnamed x22 -> x26, local copies, waits for them, and re-layouts: 2.65 us -> 7.15 us
    pallas_call x17 -> x16, Pallas kernels: 21.8 us -> 17.9 us  [call(): pl.pallas_call(body, in_specs=vmem_specs(len(args)), out_specs=vmem_specs...]
    all_to_all x8 -> x7, starting transfers between devices: 32 us -> 28.6 us  [exchange(): lax.all_to_all(tiles, AXES, 0, 0, axis_index_groups=same_core_groups(min(...]
  transfers between devices with their start and end apart: 32 -> 34, of which waited for: 22 -> 23; matrix products, arithmetic and copies ran while one was open for 1% -> 1% of each run, Pallas kernels for 4% -> 4%
where the time goes in v3:
time: 423 us; the launch traced here: 422 us
  waiting for transfers between devices  171 us (40%)
  blocking collectives  101 us (24%)
  starting transfers between devices  73 us (17%)
  Pallas kernels  63.4 us (15%)
  local copies, waits for them, and re-layouts  13 us (3%)
    all_to_all x6, blocking collectives, exchange(): lax.all_to_all(tiles, AXES, 0, 0, axis_index_groups=same_core_groups(min(...  101 us
    ppermute x22, waiting for transfers between devices, swap(): return lax.ppermute(block, AXES, [(i, i ^ mask) for i in range(count)])  75 us
    all_to_all x7, waiting for transfers between devices, exchange(): lax.all_to_all(tiles, AXES, 0, 0, axis_index_groups=same_core_groups(min(...  51 us
    all_to_all x2, waiting for transfers between devices, move_rows(): return lax.all_to_all(tiles, AXES, 0, 0, tiled=True).reshape(outgoing.shape)  36.7 us
    all_to_all x7, starting transfers between devices, exchange(): lax.all_to_all(tiles, AXES, 0, 0, axis_index_groups=same_core_groups(min(...  28.6 us
    pallas_call x7, Pallas kernels, applied(): pl.pallas_call(body, in_specs=[pl.BlockSpec(memory_space=pltpu.SMEM)] + [...  26.1 us
    ppermute x22, starting transfers between devices, swap(): return lax.ppermute(block, AXES, [(i, i ^ mask) for i in range(count)])  24.4 us
    pallas_call x16, Pallas kernels, call(): pl.pallas_call(body, in_specs=vmem_specs(len(args)), out_specs=vmem_specs...  17.9 us
  transfers between devices with their start and end apart: 34, of which 23 were waited for; matrix products, arithmetic and copies ran while one was open for 1% of the time, Pallas kernels for 4%

profile of v3, /device:TPU:1, one launch (start us, length us, event | category | flops | bytes accessed | tf_op | source)
XLA Modules:
  0.0 422.2 jit_solution(8679964841143894451)
XLA Ops:
  1.8 5.2 %shard_map.100 = (f32[384,1536]{1,0:T(8,128)}, f32[384,1024]{1,0:T(8,128)}, f32[2048,128]{1,0:T(8,128)}, s32[1,768]{1,0:T(1,128)S(1)}) custom-call(s32[6]{0:T(128)S(1)} %stack.69.at_ref, f32[384,3072]{1,0:T(8,128)} %bitcast.59, f32[384,2048]{1,0:T(8,128)} %bitcast.65, s32[1,768]{1,0:T(1,128)S(1)} %broadcast_in_dim.9.refs_2_, f32[768,128]{1,0:T(8,128)S(1)} %copy-done.4), custom_call_target="tpu_custom_call" | custom-call | tf_op jit(solution)/shard_map/pallas_call | solution.py:130
  6.9 1.5 collective-permute-start.1
  8.4 10.2 %all-to-all-start = ((f32[128,16,128]{2,1,0:T(8,128)}), f32[128,16,128]{2,1,0:T(8,128)S(1)}, u32[]{:S(2)}, u32[]{:S(2)}) async-start(f32[128,16,128]{2,1,0:T(8,128)} %bitcast.10), calls=%async_computation | async-start | bytes 2097152 | tf_op jit(solution)/shard_map/all_to_all | solution.py:360
  20.4 17.5 %all-to-all-done = f32[128,16,128]{2,1,0:T(8,128)S(1)} async-done(((f32[128,16,128]{2,1,0:T(8,128)}), f32[128,16,128]{2,1,0:T(8,128)S(1)}, u32[]{:S(2)}, u32[]{:S(2)}) %all-to-all-start) | async-done | bytes 1048608 | tf_op jit(solution)/shard_map/all_to_all | solution.py:360
  37.9 1.6 gather_fusion
  40.5 3.5 all-to-all-start.1
  44.0 11.4 %all-to-all-done.1 = f32[4,384,128]{2,1,0:T(8,128)S(1)} async-done(((f32[4,384,128]{2,1,0:T(8,128)}), f32[4,384,128]{2,1,0:T(8,128)S(1)}, u32[]{:S(2)}, u32[]{:S(2)}) %all-to-all-start.1) | async-done | bytes 786464 | tf_op jit(solution)/shard_map/all_to_all | solution.py:60
  55.3 4.5 %shard_map.102 = (f32[2,384,128]{2,1,0:T(8,128)S(1)}, f32[768,1024]{1,0:T(8,128)S(1)}) custom-call(s32[6]{0:T(128)S(1)} %stack.69.at_ref, f32[384,3072]{1,0:T(8,128)} %bitcast.60, f32[384,1536]{1,0:T(8,128)} %collective-permute-done.1.refs_1_.refs_3_, f32[384,2048]{1,0:T(8,128)} %bitcast.66, f32[384,1024]{1,0:T(8,128)} %copy-done.5, f32[1536,128]{1,0:T(8,128)S(1)} %bitcast.51), custom_call_target="tpu_custom_call" | custom-call | tf_op jit(solution)/shard_map/pallas_call | solution.py:205
  59.8 1.6 copy-done.2
  61.4 1.8 collective-permute-start.4
  63.3 6.1 %shard_map.101 = (f32[128,1024]{1,0:T(8,128)}, f32[128,2048]{1,0:T(8,128)}, f32[128,2048]{1,0:T(8,128)}, f32[128,2048]{1,0:T(8,128)}, f32[128,2048]{1,0:T(8,128)}, /*index=5*/f32[128,2048]{1,0:T(8,128)}) custom-call(s32[6]{0:T(128)S(1)} %stack.76.at_ref, f32[128,2048]{1,0:T(8,128)} %bitcast.76, f32[128,4096]{1,0:T(8,128)} %bitcast.68, f32[128,8192]{1,0:T(8,128)} %bitcast.55, ...), custom_call_target="tpu_custom_call" | custom-call | tf_op jit(solution)/shard_map/pallas_call | solution.py:130
  69.6 2.8 shard_map.103
  72.4 3.5 all-to-all-start.2
  76.5 8.5 %all-to-all-done.2.tiles_ref = f32[8,128,128]{2,1,0:T(8,128)S(1)} async-done(((f32[8,128,128]{2,1,0:T(8,128)}), f32[8,128,128]{2,1,0:T(8,128)S(1)}, u32[]{:S(2)}, u32[]{:S(2)}) %all-to-all-start.2) | async-done | bytes 524320 | tf_op jit(solution)/shard_map/all_to_all | solution.py:60
  85.8 3.5 all-to-all-start.3
  89.4 8.5 %all-to-all-done.3 = f32[8,128,128]{2,1,0:T(8,128)S(1)} async-done(((f32[8,128,128]{2,1,0:T(8,128)}), f32[8,128,128]{2,1,0:T(8,128)S(1)}, u32[]{:S(2)}, u32[]{:S(2)}) %all-to-all-start.3) | async-done | bytes 524320 | tf_op jit(solution)/shard_map/all_to_all | solution.py:60
  97.8 2.8 shard_map.106
  100.6 1.9 collective-permute-start.12
  103.5 2.8 shard_map.107
  106.3 3.7 all-to-all-start.4
  110.0 2.0 collective-permute-start.7
  112.1 3.5 shard_map.104
  116.2 10.2 %all-to-all-done.4.tiles_ref = f32[16,128,128]{2,1,0:T(8,128)S(1)} async-done(((f32[16,128,128]{2,1,0:T(8,128)}), f32[16,128,128]{2,1,0:T(8,128)S(1)}, u32[]{:S(2)}, u32[]{:S(2)}) %all-to-all-start.4) | async-done | bytes 1048608 | tf_op jit(solution)/shard_map/all_to_all | solution.py:60
  127.5 4.0 all-to-all-start.5
  131.5 3.1 collective-permute-done.6.refs_4_.refs_2_
  134.6 23.1 %collective-permute-done.7.refs_5_.refs_3_ = f32[128,2048]{1,0:T(8,128)} collective-permute-done((f32[128,2048]{1,0:T(8,128)}, f32[128,2048]{1,0:T(8,128)}, u32[]{:S(2)}, u32[]{:S(2)}) %collective-permute-start.7) | collective-permute-done | bytes 1048608 | tf_op jit(solution)/shard_map/ppermute | solution.py:67
  157.7 3.8 shard_map.109
  161.7 1.3 collective-permute-done.13.there_ref
  163.1 4.9 %collective-permute-done.14.far_ref = f32[256,128]{1,0:T(8,128)S(1)} collective-permute-done((f32[256,128]{1,0:T(8,128)S(1)}, f32[256,128]{1,0:T(8,128)S(1)}, u32[]{:S(2)}, u32[]{:S(2)}) %collective-permute-start.14) | collective-permute-done | bytes 131104 | tf_op jit(solution)/shard_map/ppermute | solution.py:67
  168.0 3.4 shard_map.111
  171.4 6.5 %all-to-all-start.6 = ((f32[16,128,128]{2,1,0:T(8,128)}), f32[16,128,128]{2,1,0:T(8,128)S(1)}, u32[]{:S(2)}, u32[]{:S(2)}) async-start(f32[16,128,128]{2,1,0:T(8,128)} %bitcast.33), calls=%async_computation.6 | async-start | bytes 2097152 | tf_op jit(solution)/shard_map/all_to_all | solution.py:60
  178.0 2.9 collective-permute-start.11
  180.9 12.4 %all-to-all-done.6.tiles_ref = f32[16,128,128]{2,1,0:T(8,128)S(1)} async-done(((f32[16,128,128]{2,1,0:T(8,128)}), f32[16,128,128]{2,1,0:T(8,128)S(1)}, u32[]{:S(2)}, u32[]{:S(2)}) %all-to-all-start.6) | async-done | bytes 1048608 | tf_op jit(solution)/shard_map/all_to_all | solution.py:60
  194.5 3.9 all-to-all-start.7
  198.4 3.3 collective-permute-done.10.refs_2_
  201.6 24.0 %collective-permute-done.11.refs_3_ = f32[128,2048]{1,0:T(8,128)} collective-permute-done((f32[128,2048]{1,0:T(8,128)}, f32[128,2048]{1,0:T(8,128)}, u32[]{:S(2)}, u32[]{:S(2)}) %collective-permute-start.11) | collective-permute-done | bytes 1048608 | tf_op jit(solution)/shard_map/ppermute | solution.py:67
  225.7 3.8 shard_map.113
  231.0 4.9 %collective-permute-done.16.there_ref = f32[2,128,128]{2,1,0:T(8,128)S(1)} collective-permute-done((f32[2,128,128]{2,1,0:T(8,128)S(1)}, f32[2,128,128]{2,1,0:T(8,128)S(1)}, u32[]{:S(2)}, u32[]{:S(2)}) %collective-permute-start.16) | collective-permute-done | bytes 131104 | tf_op jit(solution)/shard_map/ppermute | solution.py:67
  238.0 2.4 shard_map.116
  240.4 22.4 %all_to_all.75.tiles_ref = f32[16,128,128]{2,1,0:T(8,128)S(1)} all-to-all(f32[16,128,128]{2,1,0:T(8,128)S(1)} %bitcast.50), channel_id=1, replica_groups={{0,8,16,24,2,10,18,26,4,12,20,28,6,14,22,30},{1,9,17,25,3,11,19,27,5,13..., dimensions={0} | all-to-all | bytes 2097152 | tf_op jit(solution)/shard_map/all_to_all | solution.py:60
  262.9 18.3 %all_to_all.76 = f32[16,128,128]{2,1,0:T(8,128)S(1)} all-to-all(f32[16,128,128]{2,1,0:T(8,128)S(1)} %get-tuple-element.80), channel_id=1, replica_groups={{0,8,16,24,2,10,18,26,4,12,20,28,6,14,22,30},{1,9,17,25,3,11,19,27,5,13..., dimensions={0} | all-to-all | bytes 2097152 | tf_op jit(solution)/shard_map/all_to_all | solution.py:60
  281.3 3.9 shard_map.118
  285.3 3.8 collective-permute-done.18.there_ref
  289.1 4.5 %collective-permute-start.19 = (f32[2,128,128]{2,1,0:T(8,128)S(1)}, f32[2,128,128]{2,1,0:T(8,128)S(1)}, u32[]{:S(2)}, u32[]{:S(2)}) collective-permute-start(f32[2,128,128]{2,1,0:T(8,128)S(1)} %shard_map.119.here_ref), channel_id=1, source_target_pairs={{0,1},{1,0},{2,3},{3,2},{4,5},{5,4},{6,7},{7,6},{8,9},{9,8},{10,11... | collective-permute-start | bytes 393224 | tf_op jit(solution)/shard_map/ppermute | solution.py:67
  294.6 1.8 shard_map.120
  296.4 19.0 %all_to_all.77.tiles_ref = f32[16,128,128]{2,1,0:T(8,128)S(1)} all-to-all(f32[16,128,128]{2,1,0:T(8,128)S(1)} %bitcast.48), channel_id=1, replica_groups={{0,8,16,24,2,10,18,26,4,12,20,28,6,14,22,30},{1,9,17,25,3,11,19,27,5,13..., dimensions={0} | all-to-all | bytes 2097152 | tf_op jit(solution)/shard_map/all_to_all | solution.py:60
  315.5 18.3 %all_to_all.78 = f32[16,128,128]{2,1,0:T(8,128)S(1)} all-to-all(f32[16,128,128]{2,1,0:T(8,128)S(1)} %get-tuple-element.83), channel_id=1, replica_groups={{0,8,16,24,2,10,18,26,4,12,20,28,6,14,22,30},{1,9,17,25,3,11,19,27,5,13..., dimensions={0} | all-to-all | bytes 2097152 | tf_op jit(solution)/shard_map/all_to_all | solution.py:60
  333.9 3.1 shard_map.122
  337.0 3.3 collective-permute-start.20
  342.6 11.7 %all_to_all.79.tiles_ref = f32[8,128,128]{2,1,0:T(8,128)S(1)} all-to-all(f32[8,128,128]{2,1,0:T(8,128)S(1)} %bitcast.53), channel_id=1, replica_groups={{0,8,2,10,4,12,6,14},{1,9,3,11,5,13,7,15},{16,24,18,26,20,28,22,30},{17..., dimensions={0} | all-to-all | bytes 1048576 | tf_op jit(solution)/shard_map/all_to_all | solution.py:60
  354.4 11.0 %all_to_all.80 = f32[8,128,128]{2,1,0:T(8,128)S(1)} all-to-all(f32[8,128,128]{2,1,0:T(8,128)S(1)} %get-tuple-element.87), channel_id=1, replica_groups={{0,8,2,10,4,12,6,14},{1,9,3,11,5,13,7,15},{16,24,18,26,20,28,22,30},{17..., dimensions={0} | all-to-all | bytes 1048576 | tf_op jit(solution)/shard_map/all_to_all | solution.py:60
  365.4 4.2 shard_map.125
  369.6 2.2 copy-done
  371.7 2.4 collective-permute-start.21
  374.2 1.3 collective-permute-done.21.there_ref
  375.5 2.3 copy-done.1
  377.9 2.0 shard_map.126
  380.0 2.6 collective-permute-start.23
  382.6 5.0 %collective-permute-done.22 = f32[384,128]{1,0:T(8,128)S(1)} collective-permute-done((f32[384,128]{1,0:T(8,128)S(1)}, f32[384,128]{1,0:T(8,128)S(1)}, u32[]{:S(2)}, u32[]{:S(2)}) %collective-permute-start.22) | collective-permute-done | bytes 196640 | tf_op jit(solution)/shard_map/ppermute | solution.py:285
  387.6 3.3 collective-permute-done.24
  391.0 2.6 shard_map.127
  393.6 7.0 %all-to-all-start.14 = ((f32[128,16,128]{2,1,0:T(8,128)}), f32[128,16,128]{2,1,0:T(8,128)S(1)}, u32[]{:S(2)}, u32[]{:S(2)}) async-start(f32[128,16,128]{2,1,0:T(8,128)} %bitcast.41), calls=%async_computation.14 | async-start | bytes 2097152 | tf_op jit(solution)/shard_map/all_to_all | solution.py:360
  400.7 19.2 %all-to-all-done.14 = f32[128,16,128]{2,1,0:T(8,128)S(1)} async-done(((f32[128,16,128]{2,1,0:T(8,128)}), f32[128,16,128]{2,1,0:T(8,128)S(1)}, u32[]{:S(2)}, u32[]{:S(2)}) %all-to-all-start.14) | async-done | bytes 1048608 | tf_op jit(solution)/shard_map/all_to_all | solution.py:360
  419.9 2.3 gather_fusion.1
  (84 shorter events, 17.9 us)
Async XLA Ops:
  0.8 1.0 copy-start.4
  1.8 18.0 %copy-start.12 = (s32[768]{0:T(1024)S(1)}, s32[768]{0:T(1024)}, u32[]{:S(2)}) copy-start(s32[768]{0:T(1024)} %param.11) | copy-start | bytes 9220
  6.9 48.4 %collective-permute-start.1 = (f32[384,1536]{1,0:T(8,128)}, f32[384,1536]{1,0:T(8,128)}, u32[]{:S(2)}, u32[]{:S(2)}) collective-permute-start(f32[384,1536]{1,0:T(8,128)} %get-tuple-element.53), channel_id=1, source_target_pairs={{0,1},{1,0},{2,3},{3,2},{4,5},{5,4},{6,7},{7,6},{8,9},{9,8},{10,11... | collective-permute-start | bytes 7077896 | tf_op jit(solution)/shard_map/ppermute | solution.py:67
  8.4 29.5 %all-to-all-start = ((f32[128,16,128]{2,1,0:T(8,128)}), f32[128,16,128]{2,1,0:T(8,128)S(1)}, u32[]{:S(2)}, u32[]{:S(2)}) async-start(f32[128,16,128]{2,1,0:T(8,128)} %bitcast.10), calls=%async_computation | async-start | bytes 2097152 | tf_op jit(solution)/shard_map/all_to_all | solution.py:360
  18.6 25.3 %collective-permute-start = (f32[384,1024]{1,0:T(8,128)}, f32[384,1024]{1,0:T(8,128)S(1)}, u32[]{:S(2)}, u32[]{:S(2)}) collective-permute-start(f32[384,1024]{1,0:T(8,128)} %get-tuple-element.52), channel_id=1, source_target_pairs={{0,1},{1,0},{2,3},{3,2},{4,5},{5,4},{6,7},{7,6},{8,9},{9,8},{10,11... | collective-permute-start | bytes 4718600 | tf_op jit(solution)/shard_map/ppermute | solution.py:67
  39.4 20.4 %copy-start.9 = (f32[768,128]{1,0:T(8,128)}, f32[768,128]{1,0:T(8,128)S(1)}, u32[]{:S(2)}) copy-start(f32[768,128]{1,0:T(8,128)S(1)} %gather_fusion) | copy-start | bytes 1179652
  40.5 14.9 %all-to-all-start.1 = ((f32[4,384,128]{2,1,0:T(8,128)}), f32[4,384,128]{2,1,0:T(8,128)S(1)}, u32[]{:S(2)}, u32[]{:S(2)}) async-start(f32[4,384,128]{2,1,0:T(8,128)} %broadcast_in_dim.11), calls=%async_computation.1 | async-start | bytes 1572864 | tf_op jit(solution)/shard_map/all_to_all | solution.py:60
  44.0 11.4 %copy-start.5 = (f32[384,1024]{1,0:T(8,128)}, f32[384,1024]{1,0:T(8,128)S(1)}, u32[]{:S(2)}) copy-start(f32[384,1024]{1,0:T(8,128)S(1)} %collective-permute-done.refs_3_.refs_1_) | copy-start | bytes 4718596
  59.8 1.6 copy-start.2
  61.4 8.2 %collective-permute-start.4 = (f32[2,384,128]{2,1,0:T(8,128)S(1)}, f32[2,384,128]{2,1,0:T(8,128)S(1)}, u32[]{:S(2)}, u32[]{:S(2)}) collective-permute-start(f32[2,384,128]{2,1,0:T(8,128)S(1)} %get-tuple-element.61.here_ref), channel_id=1, source_target_pairs={{0,1},{1,0},{2,3},{3,2},{4,5},{5,4},{6,7},{7,6},{8,9},{9,8},{10,11... | collective-permute-start | bytes 1179656 | tf_op jit(solution)/shard_map/ppermute | solution.py:67
  63.3 6.3 %copy-start.3 = (f32[768,1024]{1,0:T(8,128)S(1)}, f32[768,1024]{1,0:T(8,128)}, u32[]{:S(2)}) copy-start(f32[768,1024]{1,0:T(8,128)} %copy-done.2) | copy-start | bytes 9437188
  69.5 19.8 %collective-permute-start.2 = (f32[128,2048]{1,0:T(8,128)}, f32[128,2048]{1,0:T(8,128)S(1)}, u32[]{:S(2)}, u32[]{:S(2)}) collective-permute-start(f32[128,2048]{1,0:T(8,128)} %get-tuple-element.57), channel_id=1, source_target_pairs={{0,1},{1,0},{2,3},{3,2},{4,5},{5,4},{6,7},{7,6},{8,9},{9,8},{10,11... | collective-permute-start | bytes 3145736 | tf_op jit(solution)/shard_map/ppermute | solution.py:67
  69.6 6.9 %copy-start.10 = (f32[768,128]{1,0:T(8,128)S(1)}, f32[768,128]{1,0:T(8,128)}, u32[]{:S(2)}) copy-start(f32[768,128]{1,0:T(8,128)} %copy-done.9) | copy-start | bytes 1179652
  72.4 12.6 %all-to-all-start.2 = ((f32[8,128,128]{2,1,0:T(8,128)}), f32[8,128,128]{2,1,0:T(8,128)S(1)}, u32[]{:S(2)}, u32[]{:S(2)}) async-start(f32[8,128,128]{2,1,0:T(8,128)} %bitcast.29), calls=%async_computation.2 | async-start | bytes 1048576 | tf_op jit(solution)/shard_map/all_to_all | solution.py:60
  75.9 13.4 %collective-permute-start.3 = (f32[128,1024]{1,0:T(8,128)}, f32[128,1024]{1,0:T(8,128)S(1)}, u32[]{:S(2)}, u32[]{:S(2)}) collective-permute-start(f32[128,1024]{1,0:T(8,128)} %get-tuple-element.58), channel_id=1, source_target_pairs={{0,1},{1,0},{2,3},{3,2},{4,5},{5,4},{6,7},{7,6},{8,9},{9,8},{10,11... | collective-permute-start | bytes 1572872 | tf_op jit(solution)/shard_map/ppermute | solution.py:67
  85.8 12.0 %all-to-all-start.3 = ((f32[8,128,128]{2,1,0:T(8,128)}), f32[8,128,128]{2,1,0:T(8,128)S(1)}, u32[]{:S(2)}, u32[]{:S(2)}) async-start(f32[8,128,128]{2,1,0:T(8,128)} %shard_map.105), calls=%async_computation.3 | async-start | bytes 1048576 | tf_op jit(solution)/shard_map/all_to_all | solution.py:60
  89.3 8.5 %copy-start.8 = (f32[128,1024]{1,0:T(8,128)}, f32[128,1024]{1,0:T(8,128)S(1)}, u32[]{:S(2)}) copy-start(f32[128,1024]{1,0:T(8,128)S(1)} %collective-permute-done.3.refs_1_.refs_3_) | copy-start | bytes 1572868
  89.3 8.5 %copy-start.7 = (f32[128,2048]{1,0:T(8,128)}, f32[128,2048]{1,0:T(8,128)S(1)}, u32[]{:S(2)}) copy-start(f32[128,2048]{1,0:T(8,128)S(1)} %collective-permute-done.2.refs_3_.refs_1_) | copy-start | bytes 3145732
  100.6 2.9 collective-permute-start.12
  106.3 20.1 %all-to-all-start.4 = ((f32[16,128,128]{2,1,0:T(8,128)}), f32[16,128,128]{2,1,0:T(8,128)S(1)}, u32[]{:S(2)}, u32[]{:S(2)}) async-start(f32[16,128,128]{2,1,0:T(8,128)} %bitcast.31), calls=%async_computation.4 | async-start | bytes 2097152 | tf_op jit(solution)/shard_map/all_to_all | solution.py:60
  109.9 24.6 %collective-permute-start.6 = (f32[128,2048]{1,0:T(8,128)}, f32[128,2048]{1,0:T(8,128)S(1)}, u32[]{:S(2)}, u32[]{:S(2)}) collective-permute-start(f32[128,2048]{1,0:T(8,128)} %get-tuple-element.66), channel_id=1, source_target_pairs={{0,32},{1,33},{2,34},{3,35},{4,36},{5,37},{6,38},{7,39},{8,40},{9,... | collective-permute-start | bytes 3145736 | tf_op jit(solution)/shard_map/ppermute | solution.py:67
  110.0 47.7 %collective-permute-start.7 = (f32[128,2048]{1,0:T(8,128)}, f32[128,2048]{1,0:T(8,128)}, u32[]{:S(2)}, u32[]{:S(2)}) collective-permute-start(f32[128,2048]{1,0:T(8,128)} %get-tuple-element.67), channel_id=1, source_target_pairs={{0,33},{1,32},{2,35},{3,34},{4,37},{5,36},{6,39},{7,38},{8,41},{9,... | collective-permute-start | bytes 3145736 | tf_op jit(solution)/shard_map/ppermute | solution.py:67
  115.6 42.1 %collective-permute-start.5 = (f32[128,2048]{1,0:T(8,128)}, f32[128,2048]{1,0:T(8,128)}, u32[]{:S(2)}, u32[]{:S(2)}) collective-permute-start(f32[128,2048]{1,0:T(8,128)} %get-tuple-element.65), channel_id=1, source_target_pairs={{0,1},{1,0},{2,3},{3,2},{4,5},{5,4},{6,7},{7,6},{8,9},{9,8},{10,11... | collective-permute-start | bytes 3145736 | tf_op jit(solution)/shard_map/ppermute | solution.py:67
  115.7 42.0 %collective-permute-start.8 = (f32[128,2048]{1,0:T(8,128)}, f32[128,2048]{1,0:T(8,128)}, u32[]{:S(2)}, u32[]{:S(2)}) collective-permute-start(f32[128,2048]{1,0:T(8,128)} %get-tuple-element.68), channel_id=1, source_target_pairs={{0,1},{1,0},{2,3},{3,2},{4,5},{5,4},{6,7},{7,6},{8,9},{9,8},{10,11... | collective-permute-start | bytes 3145736 | tf_op jit(solution)/shard_map/ppermute | solution.py:67
  127.5 30.2 %all-to-all-start.5 = ((f32[16,128,128]{2,1,0:T(8,128)}), f32[16,128,128]{2,1,0:T(8,128)S(1)}, u32[]{:S(2)}, u32[]{:S(2)}) async-start(f32[16,128,128]{2,1,0:T(8,128)} %shard_map.108), calls=%async_computation.5 | async-start | bytes 2097152 | tf_op jit(solution)/shard_map/all_to_all | solution.py:60
  134.6 23.1 %copy-start.6 = (f32[128,2048]{1,0:T(8,128)}, f32[128,2048]{1,0:T(8,128)S(1)}, u32[]{:S(2)}) copy-start(f32[128,2048]{1,0:T(8,128)S(1)} %collective-permute-done.6.refs_4_.refs_2_) | copy-start | bytes 3145732
  161.6 1.4 collective-permute-start.13
  163.0 5.0 %collective-permute-start.14 = (f32[256,128]{1,0:T(8,128)S(1)}, f32[256,128]{1,0:T(8,128)S(1)}, u32[]{:S(2)}, u32[]{:S(2)}) collective-permute-start(f32[256,128]{1,0:T(8,128)S(1)} %shard_map.110.solved_ref), channel_id=1, source_target_pairs={{0,32},{1,33},{2,34},{3,35},{4,36},{5,37},{6,38},{7,39},{8,40},{9,... | collective-permute-start | bytes 393224 | tf_op jit(solution)/shard_map/ppermute | solution.py:67
  171.4 22.0 %all-to-all-start.6 = ((f32[16,128,128]{2,1,0:T(8,128)}), f32[16,128,128]{2,1,0:T(8,128)S(1)}, u32[]{:S(2)}, u32[]{:S(2)}) async-start(f32[16,128,128]{2,1,0:T(8,128)} %bitcast.33), calls=%async_computation.6 | async-start | bytes 2097152 | tf_op jit(solution)/shard_map/all_to_all | solution.py:60
  177.9 23.7 %collective-permute-start.10 = (f32[128,2048]{1,0:T(8,128)}, f32[128,2048]{1,0:T(8,128)S(1)}, u32[]{:S(2)}, u32[]{:S(2)}) collective-permute-start(f32[128,2048]{1,0:T(8,128)} %get-tuple-element.70), channel_id=1, source_target_pairs={{0,32},{1,33},{2,34},{3,35},{4,36},{5,37},{6,38},{7,39},{8,40},{9,... | collective-permute-start | bytes 3145736 | tf_op jit(solution)/shard_map/ppermute | solution.py:67
  178.0 47.7 %collective-permute-start.11 = (f32[128,2048]{1,0:T(8,128)}, f32[128,2048]{1,0:T(8,128)}, u32[]{:S(2)}, u32[]{:S(2)}) collective-permute-start(f32[128,2048]{1,0:T(8,128)} %get-tuple-element.71), channel_id=1, source_target_pairs={{0,33},{1,32},{2,35},{3,34},{4,37},{5,36},{6,39},{7,38},{8,41},{9,... | collective-permute-start | bytes 3145736 | tf_op jit(solution)/shard_map/ppermute | solution.py:67
  180.9 44.8 %collective-permute-start.9 = (f32[128,2048]{1,0:T(8,128)}, f32[128,2048]{1,0:T(8,128)}, u32[]{:S(2)}, u32[]{:S(2)}) collective-permute-start(f32[128,2048]{1,0:T(8,128)} %get-tuple-element.69), channel_id=1, source_target_pairs={{0,1},{1,0},{2,3},{3,2},{4,5},{5,4},{6,7},{7,6},{8,9},{9,8},{10,11... | collective-permute-start | bytes 3145736 | tf_op jit(solution)/shard_map/ppermute | solution.py:67
  194.5 31.2 %all-to-all-start.7 = ((f32[16,128,128]{2,1,0:T(8,128)}), f32[16,128,128]{2,1,0:T(8,128)S(1)}, u32[]{:S(2)}, u32[]{:S(2)}) async-start(f32[16,128,128]{2,1,0:T(8,128)} %shard_map.112), calls=%async_computation.7 | async-start | bytes 2097152 | tf_op jit(solution)/shard_map/all_to_all | solution.py:60
  201.6 24.0 %copy-start.11 = (f32[128,2048]{1,0:T(8,128)}, f32[128,2048]{1,0:T(8,128)S(1)}, u32[]{:S(2)}) copy-start(f32[128,2048]{1,0:T(8,128)S(1)} %collective-permute-done.10.refs_2_) | copy-start | bytes 3145732
  229.5 1.4 collective-permute-start.15
  230.9 5.0 %collective-permute-start.16 = (f32[2,128,128]{2,1,0:T(8,128)S(1)}, f32[2,128,128]{2,1,0:T(8,128)S(1)}, u32[]{:S(2)}, u32[]{:S(2)}) collective-permute-start(f32[2,128,128]{2,1,0:T(8,128)S(1)} %shard_map.114.here_ref), channel_id=1, source_target_pairs={{0,32},{1,33},{2,34},{3,35},{4,36},{5,37},{6,38},{7,39},{8,40},{9,... | collective-permute-start | bytes 393224 | tf_op jit(solution)/shard_map/ppermute | solution.py:67
  235.9 2.1 collective-permute-start.17
  285.2 3.9 collective-permute-start.18
  289.1 5.5 %collective-permute-start.19 = (f32[2,128,128]{2,1,0:T(8,128)S(1)}, f32[2,128,128]{2,1,0:T(8,128)S(1)}, u32[]{:S(2)}, u32[]{:S(2)}) collective-permute-start(f32[2,128,128]{2,1,0:T(8,128)S(1)} %shard_map.119.here_ref), channel_id=1, source_target_pairs={{0,1},{1,0},{2,3},{3,2},{4,5},{5,4},{6,7},{7,6},{8,9},{9,8},{10,11... | collective-permute-start | bytes 393224 | tf_op jit(solution)/shard_map/ppermute | solution.py:67
  337.0 4.3 %collective-permute-start.20 = (f32[2,128,128]{2,1,0:T(8,128)S(1)}, f32[2,128,128]{2,1,0:T(8,128)S(1)}, u32[]{:S(2)}, u32[]{:S(2)}) collective-permute-start(f32[2,128,128]{2,1,0:T(8,128)S(1)} %get-tuple-element.85.here_ref), channel_id=1, source_target_pairs={{0,1},{1,0},{2,3},{3,2},{4,5},{5,4},{6,7},{7,6},{8,9},{9,8},{10,11... | collective-permute-start | bytes 393224 | tf_op jit(solution)/shard_map/ppermute | solution.py:67
  369.6 2.2 copy-start
  371.7 3.8 collective-permute-start.21
  375.5 2.3 copy-start.1
  379.9 7.8 %collective-permute-start.22 = (f32[384,128]{1,0:T(8,128)S(1)}, f32[384,128]{1,0:T(8,128)S(1)}, u32[]{:S(2)}, u32[]{:S(2)}) collective-permute-start(f32[384,128]{1,0:T(8,128)S(1)} %get-tuple-element.92), channel_id=1, source_target_pairs={{0,2},{1,3},{2,4},{3,5},{4,6},{5,7},{6,0},{7,1},{8,10},{9,11},{10,... | collective-permute-start | bytes 589832 | tf_op jit(solution)/shard_map/ppermute | solution.py:285
  380.0 7.7 %collective-permute-start.23 = (f32[384,128]{1,0:T(8,128)S(1)}, f32[384,128]{1,0:T(8,128)S(1)}, u32[]{:S(2)}, u32[]{:S(2)}) collective-permute-start(f32[384,128]{1,0:T(8,128)S(1)} %get-tuple-element.93), channel_id=1, source_target_pairs={{0,6},{1,7},{2,0},{3,1},{4,2},{5,3},{6,4},{7,5},{8,14},{9,15},{10,... | collective-permute-start | bytes 589832 | tf_op jit(solution)/shard_map/ppermute | solution.py:285
  382.6 8.3 %collective-permute-start.24 = (f32[384,128]{1,0:T(8,128)S(1)}, f32[384,128]{1,0:T(8,128)S(1)}, u32[]{:S(2)}, u32[]{:S(2)}) collective-permute-start(f32[384,128]{1,0:T(8,128)S(1)} %get-tuple-element.94), channel_id=1, source_target_pairs={{0,4},{1,5},{2,6},{3,7},{4,0},{5,1},{6,2},{7,3},{8,12},{9,13},{10,... | collective-permute-start | bytes 589832 | tf_op jit(solution)/shard_map/ppermute | solution.py:285
  393.6 26.3 %all-to-all-start.14 = ((f32[128,16,128]{2,1,0:T(8,128)}), f32[128,16,128]{2,1,0:T(8,128)S(1)}, u32[]{:S(2)}, u32[]{:S(2)}) async-start(f32[128,16,128]{2,1,0:T(8,128)} %bitcast.41), calls=%async_computation.14 | async-start | bytes 2097152 | tf_op jit(solution)/shard_map/all_to_all | solution.py:360
